TPU v7x, 256 devices: a whole 4x4x8 slice. The times are simulated.
256 devices in a mesh: span: 64 (over y, x, z_lo, core), head: 4 (over z_hi).
Axes of the slice: x: 4, y: 4, z: 8 (z_hi: 4, z_lo: 2; z = z_hi * 2 + z_lo), core: 2. Of those that a mesh axis runs over, the one named last changes fastest.
Arguments:
- decoder_states: bfloat16 [131072, 1024], P('span'), may hold values from -21 to 21
- encodings: bfloat16 [4096, 128, 1024], P('span', 'head'), may hold values from -21 to 21
- neighbor_table: int32 [2048, 2, 2], P('span'), may hold values from 0 to 63, as said below
- query_weight: bfloat16 [1024, 1024], P(None, 'head'), may hold values from -0.1875 to 0.1875
- key_weight: bfloat16 [1024, 1024], P(None, 'head'), may hold values from -0.1875 to 0.1875
- value_weight: bfloat16 [1024, 1024], P(None, 'head'), may hold values from -0.1875 to 0.1875
- out_weight: bfloat16 [1024, 1024], P('head'), may hold values from -0.1875 to 0.1875
Outputs:
- attended: bfloat16 [131072, 1024], P('span', 'head')
Inputs may be any that keep to these rules, and one draw needn't show every extreme that they name: neighbor_table[c, k, 0] is the database shard and neighbor_table[c, k, 1] the slot in that shard of neighbor k of span c; in each aligned block of 32 spans (the spans of one device along `span`) every shard is named by exactly one neighbor, and every slot of every shard is named exactly once in the whole table.
All inputs are finite; a program needn't handle non-finite values.
Results may differ from a plain program's by a relative error of at most 0.012.
The roundings to bfloat16 on the way count: a program that leaves them out, or rounds other values in their place, can miss the bound.
Values may be sent and summed in bfloat16 or wider, within the bound.
A program may use at most 128 MiB of HBM per device.

v0:
```python
import jax
import jax.numpy as jnp
from jax import lax
from jax.sharding import PartitionSpec as P

HEAD_DIM = 64
SPAN_LEN = 64
SEQ_LEN = 2048


def body(
    decoder_states, encodings, neighbor_table, query_weight, key_weight, value_weight, out_weight
):
    peer_count = lax.axis_size("span")
    column_rows = lax.all_to_all(out_weight, "head", split_axis=1, concat_axis=0, tiled=True)
    shard_ids = neighbor_table[:, :, 0].reshape(-1)
    slot_ids = neighbor_table[:, :, 1].reshape(-1)
    entries = shard_ids.shape[0]
    per_peer = entries // peer_count
    numbering = jnp.arange(entries, dtype=jnp.int32)
    same_before = (shard_ids[:, None] == shard_ids[None, :]) & (
        numbering[None, :] < numbering[:, None]
    )
    ranking = jnp.sum(same_before.astype(jnp.int32), axis=1)
    position = shard_ids * per_peer + ranking
    placed = position[None, :] == numbering[:, None]
    request = jnp.sum(jnp.where(placed, slot_ids[None, :], 0), axis=1)
    wanted = lax.all_to_all(request, "span", split_axis=0, concat_axis=0, tiled=True)
    selected = encodings[wanted]
    model_width = decoder_states.shape[1]
    group_cols = query_weight.shape[1]
    both_weights = jnp.concatenate([key_weight, value_weight], axis=1)
    arrived = lax.all_to_all(selected, "span", split_axis=0, concat_axis=0, tiled=True)
    block_in = lax.all_gather(arrived, "head", axis=1, tiled=True)
    flattened = block_in.reshape(-1, model_width)
    result = jnp.dot(flattened, both_weights, preferred_element_type=jnp.float32).astype(
        jnp.bfloat16
    )
    projected = result.reshape(block_in.shape[0], block_in.shape[1], 2 * group_cols)
    ordered = projected[position]
    span_count = neighbor_table.shape[0]
    neighbors = neighbor_table.shape[1]
    heads_here = group_cols // HEAD_DIM
    ordered = ordered.reshape(span_count, neighbors * projected.shape[1], 2 * group_cols)
    key_rows = ordered[:, :, :group_cols].reshape(span_count, -1, heads_here, HEAD_DIM)
    value_rows = ordered[:, :, group_cols:].reshape(span_count, -1, heads_here, HEAD_DIM)
    queries = jnp.dot(decoder_states, query_weight, preferred_element_type=jnp.float32).astype(
        jnp.bfloat16
    )
    sequences = decoder_states.shape[0] // SEQ_LEN
    offset = SPAN_LEN - 1
    queries = queries.reshape(sequences, SEQ_LEN, group_cols)
    shifted = jnp.concatenate(
        [queries[:, offset:], jnp.zeros((sequences, offset, group_cols), jnp.bfloat16)], axis=1
    )
    shifted = shifted.reshape(span_count, SPAN_LEN, heads_here, HEAD_DIM)
    inv_root = HEAD_DIM ** (-0.5)
    scores = (
        jnp.einsum("cqhd,ckhd->chqk", shifted, key_rows, preferred_element_type=jnp.float32)
        * inv_root
    )
    weights = jax.nn.softmax(scores, axis=-1).astype(jnp.bfloat16)
    context = jnp.einsum(
        "chqk,ckhd->cqhd", weights, value_rows, preferred_element_type=jnp.float32
    ).astype(jnp.bfloat16)
    context = context.reshape(sequences, SEQ_LEN, group_cols)
    context = jnp.concatenate(
        [jnp.zeros((sequences, offset, group_cols), jnp.bfloat16), context[:, : SEQ_LEN - offset]],
        axis=1,
    )
    context = context.reshape(-1, group_cols)
    summed = jnp.dot(
        lax.all_gather(context, "head", axis=1, tiled=True),
        column_rows,
        preferred_element_type=jnp.float32,
    )
    return summed.astype(jnp.bfloat16)


def solution(mesh):
    return jax.shard_map(
        body,
        mesh=mesh,
        in_specs=(
            P("span", None),
            P("span", "head", None),
            P("span", None, None),
            P(None, "head"),
            P(None, "head"),
            P(None, "head"),
            P("head", None),
        ),
        out_specs=P("span", "head"),
        check_vma=False,
    )
```

profile of v0, /device:TPU:33, one launch (start us, length us, event | category | flops | bytes accessed | tf_op | source)
XLA Modules:
  0.0 560.3 jit_solution(16839109739039627777)
XLA Ops:
  6.5 0.0 copy-start
  6.5 0.0 all-gather.4.cloned.1.call-start
  6.5 0.8 fusion.30
  7.3 0.1 copy.50
  7.4 0.1 reshape_squeeze.5
  7.5 0.2 convert_reduce_fusion
  7.7 0.1 copy.51
  7.8 0.1 broadcast_in_dim.14
  7.9 0.1 select_reduce_fusion
  8.0 0.1 copy.52
  8.1 15.8 %all_to_all.36 = s32[64,1,1]{2,1,0:T(1,128)S(1)} all-to-all(s32[64,1,1]{2,1,0:T(1,128)S(1)} %copy.52), channel_id=1, replica_groups=mesh['span'=64,'head'=4] {'span'}, dimensions={0} | all-to-all | bytes 512 | tf_op jit(solution)/shard_map/all_to_all | solution.py:28
  23.9 1.2 reduce
  25.1 4.9 gather_fusion
  30.1 56.3 %all_to_all.37 = bf16[64,32,1024]{2,1,0:T(8,128)(2,1)} all-to-all(bf16[64,32,1024]{2,1,0:T(8,128)(2,1)} %gather_fusion), channel_id=1, replica_groups=mesh['span'=64,'head'=4] {'span'}, dimensions={0} | all-to-all | bytes 8388608 | tf_op jit(solution)/shard_map/all_to_all | solution.py:33
  86.4 0.0 all-gather.4.cloned.1.call-update
  86.4 0.2 all-gather.6.cloned.1.call-start
  86.6 0.1 reshape_squeeze.6
  86.7 0.0 copy-done
  86.7 3.4 fusion.11
  90.2 0.0 copy-start.4
  90.2 0.2 slice.29
  90.4 1.0 concatenate.10
  91.5 3.3 reshape.100
  94.8 285.4 %all-gather.4.cloned.1.call-done = bf16[64,128,1024]{2,1,0:T(8,128)(2,1)} async-done(((bf16[64,32,1024]{2,1,0:T(8,128)(2,1)}), bf16[64,128,1024]{2,1,0:T(8,128)(2,1)}) %all-gather.4.cloned.1.call-update) | async-done | bytes 16777232 | tf_op jit(solution)/shard_map/all_gather | solution.py:34
  380.3 0.0 copy-done.4
  380.3 14.5 %convolution_convert_fusion = bf16[8192,512]{1,0:T(8,128)(2,1)} fusion(bf16[8192,1024]{1,0:T(8,128)(2,1)} %bitcast.54, bf16[1024,256]{1,0:T(8,128)(2,1)S(1)} %copy-done.4, bf16[1024,256]{1,0:T(8,128)(2,1)} %param.11), kind=kOutput, calls=%fused_computation.3 | convolution fusion | flops 8596226048 | bytes 26214400 | tf_op jit(solution)/shard_map/dot_general | solution.py:36
  394.8 8.9 %gather_fusion.1 = bf16[64,128,512]{2,1,0:T(8,128)(2,1)} fusion(bf16[64,128,512]{2,1,0:T(8,128)(2,1)} %bitcast.47, s32[1024]{0:T(1024)S(1)} %pad_clamp_fusion), kind=kCustom, calls=%fused_computation.1 | custom fusion | bytes 16777472 | tf_op jit(solution)/shard_map/gather | solution.py:40
  403.7 5.9 %fusion.29 = (bf16[32,256,256]{2,1,0:T(8,128)(2,1)}, bf16[32,256,256]{2,1,0:T(8,128)(2,1)}) fusion(bf16[32,256,512]{2,1,0:T(8,128)(2,1)} %bitcast.45), kind=kLoop, calls=%fused_computation.37 | loop fusion | bytes 16777216 | tf_op jit(solution)/shard_map/slice | solution.py:45
  409.6 6.4 %copy.61 = bf16[32,256,256]{1,2,0:T(8,128)(2,1)} copy(bf16[32,256,256]{2,1,0:T(8,128)(2,1)} %get-tuple-element.5) | data formatting | bytes 8388608
  416.0 3.4 fusion.12
  419.4 0.0 copy-start.2
  419.4 3.1 fusion.31
  422.6 0.1 copy-done.2
  422.6 6.4 %copy.60 = bf16[32,256,256]{1,2,0:T(8,128)(2,1)} copy(bf16[32,256,256]{2,1,0:T(8,128)(2,1)} %get-tuple-element.6) | data formatting | bytes 8388608
  429.0 22.4 %convert_bitcast_fusion = bf16[32,64,4,64]{1,3,2,0:T(8,128)(2,1)} fusion(bf16[32,256,4,64]{1,3,2,0:T(8,128)(2,1)} %bitcast.49, f32[32,4,64]{2,1,0:T(4,128)S(1)} %fusion.31, f32[32,4,64,256]{3,2,1,0:T(8,128)} %copy-done.2), kind=kOutput, calls=%fused_computation.17 | convolution fusion | flops 279453952 | bytes 13664256 | tf_op jit(solution)/shard_map/chqk,ckhd->cqhd/dot_general | solution.py:63
  451.4 2.9 copy.57
  454.4 0.0 copy-start.3
  454.4 2.4 reshape.102
  456.8 2.6 concatenate.11
  459.4 0.0 all-gather.6.cloned.1.call-update
  459.5 0.0 copy-done.3
  459.5 0.2 copy.58
  459.7 16.1 %all_to_all.38 = bf16[256,4,256]{0,2,1:T(8,128)(2,1)S(1)} all-to-all(bf16[256,4,256]{0,2,1:T(8,128)(2,1)S(1)} %bitcast.51), channel_id=1, replica_groups=mesh['span'=64,'head'=4] {'head'}, dimensions={1} | all-to-all | bytes 1048576 | tf_op jit(solution)/shard_map/all_to_all | solution.py:15
  475.8 0.2 copy.59
  476.0 72.9 %all-gather.6.cloned.1.call-done = bf16[1,2048,1024]{1,2,0:T(8,128)(2,1)} async-done(((bf16[1,2048,256]{1,2,0:T(8,128)(2,1)}), bf16[1,2048,1024]{1,2,0:T(8,128)(2,1)}) %all-gather.6.cloned.1.call-update) | async-done | bytes 4194320 | tf_op jit(solution)/shard_map/all_gather | solution.py:73
  548.9 0.0 copy-start.1
  548.9 4.5 fusion.8
  553.4 0.0 copy-done.1
  (5 shorter events, 0.0 us)
Async XLA Ops:
  6.5 80.2 %copy-start = (bf16[1024,256]{1,0:T(8,128)(2,1)S(1)}, bf16[1024,256]{1,0:T(8,128)(2,1)}, u32[]{:S(2)}) copy-start(bf16[1024,256]{1,0:T(8,128)(2,1)} %param.10) | copy-start | bytes 1572868
  6.5 373.7 %all-gather.4.cloned.1.call-start = ((), (), s32[]{:S(2)}) async-start(), calls=%async_computation.3 | async-start | bytes 20971520 | tf_op jit(solution)/shard_map/all_gather | solution.py:34
  86.4 462.5 %all-gather.6.cloned.1.call-start = ((), (), s32[]{:S(2)}) async-start(), calls=%async_computation.4 | async-start | bytes 5242880 | tf_op jit(solution)/shard_map/all_gather | solution.py:73
  90.2 290.1 %copy-start.4 = (bf16[1024,256]{1,0:T(8,128)(2,1)S(1)}, bf16[1024,256]{1,0:T(8,128)(2,1)}, u32[]{:S(2)}) copy-start(bf16[1024,256]{1,0:T(8,128)(2,1)} %param.12) | copy-start | bytes 1572868
  419.4 3.2 copy-start.2
  454.4 5.1 copy-start.3
  548.9 4.6 copy-start.1
Sparse Core Ops, SparseCore 0:
  86.5 293.6 all-gather.3
  459.6 89.2 all-gather.5
where the time goes:
time: 561 us; the launch traced here: 560 us
  waiting for transfers between devices  358 us (64%)
  blocking collectives  88.2 us (16%)
  matrix products  48.3 us (9%)
  local copies, waits for them, and re-layouts  47 us (8%)
  between operations  13.5 us (2%)
    all_gather x1, waiting for transfers between devices, body(): block_in = lax.all_gather(arrived, 'head', axis=1, tiled=True)  285 us
    all_gather x1, waiting for transfers between devices, body(): lax.all_gather(context, 'head', axis=1, tiled=True)  72.9 us
    all_to_all x1, blocking collectives, body(): lax.all_to_all(selected, 'span', split_axis=0, concat_axis=0, tiled=True)  56.3 us
    dot_general x1, matrix products, body(): jnp.einsum('chqk,ckhd->cqhd', weights, value_rows, preferred_element_type...  22.4 us
    all_to_all x1, blocking collectives, body(): lax.all_to_all(out_weight, 'head', split_axis=1, concat_axis=0, tiled=True)  16.1 us
    all_to_all x1, blocking collectives, body(): lax.all_to_all(request, 'span', split_axis=0, concat_axis=0, tiled=True)  15.8 us
    dot_general x1, matrix products, body(): jnp.dot(flattened, both_weights, preferred_element_type=jnp.float32)  14.5 us
    unnamed x13, local copies, waits for them, and re-layouts  13.1 us
  transfers between devices with their start and end apart: 2, of which 2 were waited for; matrix products, arithmetic and copies ran while one was open for 2% of the time, Pallas kernels for 0%

commit v1 on v0

v1 whole, which is shorter than its diff:
```python
import functools

import jax
import jax.numpy as jnp
from jax import lax
from jax.experimental import pallas as pl
from jax.experimental.pallas import tpu as pltpu
from jax.sharding import PartitionSpec as P

HEAD_DIM = 64
SPAN_LEN = 64
SEQ_LEN = 2048
D = 1024
HEADS = 16
SPANS = 32
OFFSET = SPAN_LEN - 1
GROUP = 256
F32 = jnp.float32
BF16 = jnp.bfloat16


def head_mask(rows, cols):
    r = lax.broadcasted_iota(jnp.int32, (rows, cols), 0) // HEAD_DIM
    c = lax.broadcasted_iota(jnp.int32, (rows, cols), 1) // HEAD_DIM
    return r == c


def attention_kernel(ids, q_ref, a_ref, b_ref, ctx_ref, lse_ref):
    mask = head_mask(GROUP, GROUP)
    ones = jnp.where(mask, 1.0, 0.0).astype(BF16)
    lane = lax.broadcasted_iota(jnp.int32, (SPAN_LEN, 128), 1)
    low = lane < HEAD_DIM
    lses = jnp.zeros((SPAN_LEN, 128), F32)
    for g in range(D // GROUP):
        cols = slice(g * GROUP, (g + 1) * GROUP)
        vcols = slice(D + g * GROUP, D + (g + 1) * GROUP)
        k4 = jnp.concatenate([a_ref[0, :, cols], b_ref[0, :, cols]], axis=0)
        v4 = jnp.concatenate([a_ref[0, :, vcols], b_ref[0, :, vcols]], axis=0)
        zero = jnp.zeros((GROUP, GROUP), BF16)
        kbd = jnp.where(mask, jnp.concatenate([k4] * 4, axis=0), zero)
        vbd = jnp.where(mask, jnp.concatenate([v4] * 4, axis=0), zero)
        s = lax.dot_general(
            q_ref[:, cols], kbd, (((1,), (1,)), ((), ())), preferred_element_type=F32
        ) * (HEAD_DIM ** -0.5)
        tops = []
        for half in range(2):
            part = s[:, half * 128 : (half + 1) * 128]
            m0 = jnp.max(jnp.where(low, part, -jnp.inf), axis=1, keepdims=True)
            m1 = jnp.max(jnp.where(low, -jnp.inf, part), axis=1, keepdims=True)
            tops.append(jnp.where(low, m0, m1))
        top = jnp.concatenate(tops, axis=1)
        p = jnp.exp(s - top).astype(BF16)
        total = jnp.dot(p, ones, preferred_element_type=F32)
        c = jnp.dot(p, vbd, preferred_element_type=F32)
        ctx_ref[:, cols] = (c / total).astype(BF16)
        lse = top + jnp.log(total)
        for n in range(4):
            lses = jnp.where(lane == g * 4 + n, lse[:, n * 64 : n * 64 + 1], lses)
    lse_ref[...] = lses[:, :HEADS]


def attention(ids, queries, projected):
    spec = pltpu.PrefetchScalarGridSpec(
        num_scalar_prefetch=1,
        grid=(SPANS,),
        in_specs=[
            pl.BlockSpec((SPAN_LEN, D), lambda j, ids: (j, 0)),
            pl.BlockSpec((1, 32, 2 * D), lambda j, ids: (ids[2 * j], 0, 0)),
            pl.BlockSpec((1, 32, 2 * D), lambda j, ids: (ids[2 * j + 1], 0, 0)),
        ],
        out_specs=[
            pl.BlockSpec((SPAN_LEN, D), lambda j, ids: (j, 0)),
            pl.BlockSpec((SPAN_LEN, HEADS), lambda j, ids: (j, 0)),
        ],
    )
    return pl.pallas_call(
        attention_kernel,
        grid_spec=spec,
        out_shape=[
            jax.ShapeDtypeStruct((SEQ_LEN, D), BF16),
            jax.ShapeDtypeStruct((SEQ_LEN, HEADS), F32),
        ],
        cost_estimate=pl.CostEstimate(
            flops=8 * SEQ_LEN * D * GROUP, bytes_accessed=16 << 20, transcendentals=1 << 21
        ),
    )(ids, queries, projected, projected)


def body(
    decoder_states, encodings, neighbor_table, query_weight, key_weight, value_weight, out_weight
):
    s = lax.axis_index("span")
    h = lax.axis_index("head")
    shard_ids = neighbor_table[:, :, 0].reshape(-1)
    slot_ids = neighbor_table[:, :, 1].reshape(-1)
    numbering = jnp.arange(64, dtype=jnp.int32)
    placed = shard_ids[None, :] == numbering[:, None]
    request = jnp.sum(jnp.where(placed, slot_ids[None, :], 0), axis=1)
    wanted = lax.all_to_all(request, "span", split_axis=0, concat_axis=0, tiled=True)

    column_pieces = [
        lax.dynamic_slice_in_dim(w, s * 16, 16, 0)
        for w in (query_weight, key_weight, value_weight)
    ]
    small = lax.all_gather(jnp.concatenate(column_pieces, axis=0), "head", axis=1, tiled=True)
    out_piece = lax.dynamic_slice_in_dim(out_weight, s * 4, 4, 0)
    out_small = lax.all_gather(out_piece, "head", axis=0, tiled=True)
    pieces = jnp.concatenate([small, out_small], axis=0)
    whole = lax.all_gather(pieces, "span", axis=0)

    selected = encodings[wanted]
    arrived = lax.all_to_all(selected, "span", split_axis=0, concat_axis=0, tiled=True)

    whole_q = whole[:, 0:16].reshape(D, D)
    whole_k = whole[:, 16:32].reshape(D, D)
    whole_v = whole[:, 32:48].reshape(D, D)
    whole_o = whole[:, 48:64].reshape(64, 4, 4, D).transpose(1, 0, 2, 3).reshape(D, D)

    shifted = jnp.concatenate(
        [decoder_states[OFFSET:], jnp.zeros((OFFSET, D), BF16)], axis=0
    )
    queries = jnp.dot(shifted, whole_q, preferred_element_type=F32).astype(BF16)
    both = jnp.concatenate([whole_k, whole_v], axis=1)
    projected = jnp.dot(
        arrived.reshape(-1, D), both, preferred_element_type=F32
    ).astype(BF16).reshape(64, 32, 2 * D)
    ctx, lse = attention(shard_ids, queries, projected)
    all_lse = lax.all_gather(lse, "head", axis=0)
    share = jnp.exp(lse - jax.nn.logsumexp(all_lse, axis=0))
    share = jnp.repeat(share, HEAD_DIM, axis=1)
    scaled = (ctx.astype(F32) * share).astype(BF16)
    partial = jnp.dot(scaled, whole_o, preferred_element_type=F32).astype(BF16)
    partial = jnp.concatenate([jnp.zeros((OFFSET, D), BF16), partial[: SEQ_LEN - OFFSET]], axis=0)
    return lax.psum_scatter(partial, "head", scatter_dimension=1, tiled=True)


def solution(mesh):
    return jax.shard_map(
        body,
        mesh=mesh,
        in_specs=(
            P("span", None),
            P("span", "head", None),
            P("span", None, None),
            P(None, "head"),
            P(None, "head"),
            P(None, "head"),
            P("head", None),
        ),
        out_specs=P("span", "head"),
        check_vma=False,
    )
```

time: 561 us -> 461 us (0.82)
  the two profiles are of different devices: /device:TPU:33 before, /device:TPU:20 now
where the time goes in v1:
time: 461 us; the launch traced here: 459 us
  waiting for transfers between devices  201 us (44%)
  blocking collectives  121 us (26%)
  local copies, waits for them, and re-layouts  42.6 us (9%)
  Pallas kernels  33.6 us (7%)
  matrix products  29.2 us (6%)
  between operations  13.5 us (3%)
  starting transfers between devices  9.42 us (2%)
  other arithmetic  8.1 us (2%)
    all_gather x1, waiting for transfers between devices, body(): whole = lax.all_gather(pieces, 'span', axis=0)  117 us
    reduce_scatter x1, waiting for transfers between devices, body(): return lax.psum_scatter(partial, 'head', scatter_dimension=1, tiled=True)  84.1 us
    all_gather x1, blocking collectives, body(): all_lse = lax.all_gather(lse, 'head', axis=0)  77.7 us
    pallas_call x1, Pallas kernels, attention(): pl.pallas_call(attention_kernel, grid_spec=spec, out_shape=[jax.ShapeDtyp...  33.6 us
    all_gather x1, blocking collectives, body(): lax.all_gather(jnp.concatenate(column_pieces, axis=0), 'head', axis=1, ti...  17.3 us
    all_gather x1, blocking collectives, body(): out_small = lax.all_gather(out_piece, 'head', axis=0, tiled=True)  13.7 us
    dot_general x1, matrix products, body(): jnp.dot(arrived.reshape(-1, D), both, preferred_element_type=F32)  13.4 us
    all_to_all x1, blocking collectives, body(): lax.all_to_all(request, 'span', split_axis=0, concat_axis=0, tiled=True)  12.6 us
  transfers between devices with their start and end apart: 3, of which 2 were waited for; matrix products, arithmetic and copies ran while one was open for 5% of the time, Pallas kernels for 0%

profile of v1, /device:TPU:20, one launch (start us, length us, event | category | flops | bytes accessed | tf_op | source)
XLA Modules:
  0.0 458.9 jit_solution(1114905239056500579)
XLA Ops:
  6.5 0.0 copy-start
  6.5 0.0 all-gather.5.cloned.1.call-start
  6.5 1.0 copy-done
  7.6 0.7 constant_dynamic-slice_fusion
  8.3 17.3 %all_gather.18 = bf16[48,1024]{1,0:T(8,128)(2,1)S(1)} all-gather(bf16[48,256]{1,0:T(8,128)(2,1)S(1)} %pad_maximum_fusion.1), channel_id=1, replica_groups=mesh['span'=64,'head'=4] {'head'}, dimensions={1}, use_global_device_ids=true | all-gather | bytes 122880 | tf_op jit(solution)/shard_map/all_gather | solution.py:105
  25.6 0.7 dynamic-slice_bitcast_fusion
  26.4 13.7 %all-gather.2 = bf16[4,4,1024]{2,1,0:T(4,128)(2,1)S(1)} all-gather(bf16[1,4,1024]{2,1,0:T(4,128)(2,1)S(1)} %dynamic-slice_bitcast_fusion), channel_id=1, replica_groups=mesh['span'=64,'head'=4] {'head'}, dimensions={0}, use_global_device_ids=true | all-gather | bytes 40960 | tf_op jit(solution)/shard_map/all_gather | solution.py:107
  40.1 0.7 pad_maximum_fusion
  40.8 0.0 all-gather.5.cloned.1.call-update
  40.8 0.8 fusion.13
  41.5 0.1 copy.39
  41.6 0.1 reshape_squeeze.3.ids
  41.7 0.0 copy-start.5
  41.7 0.1 copy.40
  41.8 0.1 broadcast_in_dim.23
  41.9 0.1 select_reduce_fusion
  42.1 0.1 copy.41
  42.2 12.6 %all_to_all.17 = s32[64,1,1]{2,1,0:T(1,128)S(1)} all-to-all(s32[64,1,1]{2,1,0:T(1,128)S(1)} %copy.41), channel_id=1, replica_groups=mesh['span'=64,'head'=4] {'span'}, dimensions={0} | all-to-all | bytes 512 | tf_op jit(solution)/shard_map/all_to_all | solution.py:99
  54.8 1.2 reduce
  56.0 5.0 %gather_fusion = bf16[64,32,1024]{2,1,0:T(8,128)(2,1)} fusion(bf16[64,32,1024]{2,1,0:T(8,128)(2,1)} %param.8, s32[1024]{0:T(1024)S(1)} %pad_clamp_fusion), kind=kCustom, calls=%fused_computation | custom fusion | bytes 8388864 | tf_op jit(solution)/shard_map/gather | solution.py:111
  61.1 0.0 copy-done.5
  61.1 9.2 %all-to-all-start.1 = ((bf16[64,32,1024]{2,1,0:T(8,128)(2,1)}), bf16[64,32,1024]{2,1,0:T(8,128)(2,1)}, u32[]{:S(2)}, u32[]{:S(2)}) async-start(bf16[64,32,1024]{2,1,0:T(8,128)(2,1)} %gather_fusion), calls=%async_computation.1 | async-start | bytes 8388608 | tf_op jit(solution)/shard_map/all_to_all | solution.py:112
  70.3 0.2 reduce-scatter.2.cloned.1.call-start
  70.5 5.3 %slice.25 = bf16[1985,1024]{1,0:T(8,128)(2,1)} slice(bf16[2048,1024]{1,0:T(8,128)(2,1)} %param.7), slice={[63:2048], [0:1024]} | slice | bytes 8130560 | tf_op jit(solution)/shard_map/slice | solution.py:120
  75.8 116.9 %all-gather.5.cloned.1.call-done = bf16[4096,1024]{1,0:T(8,128)(2,1)} async-done(((bf16[64,1024]{1,0:T(8,128)(2,1)}), bf16[4096,1024]{1,0:T(8,128)(2,1)}) %all-gather.5.cloned.1.call-update) | async-done | bytes 8388624 | tf_op jit(solution)/shard_map/all_gather | solution.py:109
  192.8 0.0 copy-start.4
  192.8 5.5 %fusion.12 = (bf16[64,16,1024]{2,1,0:T(8,128)(2,1)S(1)}, bf16[64,16,1024]{2,1,0:T(8,128)(2,1)}, bf16[64,16,1024]{2,1,0:T(8,128)(2,1)}, bf16[64,16,1024]{2,1,0:T(8,128)(2,1)S(1)}) fusion(bf16[64,64,1024]{2,1,0:T(8,128)(2,1)} %bitcast.30), kind=kLoop, calls=%fused_computation.27 | loop fusion | bytes 16777216 | tf_op jit(solution)/shard_map/slice | solution.py:115
  198.3 0.5 copy-done.4
  198.8 6.0 %fusion.6.q_ref = bf16[2048,1024]{1,0:T(8,128)(2,1)} fusion(bf16[1024,1024]{1,0:T(8,128)(2,1)S(1)} %bitcast.34, bf16[1985,1024]{1,0:T(8,128)(2,1)S(1)} %copy-done.4), kind=kOutput, calls=%fused_computation.11 | convolution fusion | flops 4297064448 | bytes 10356736 | tf_op jit(solution)/shard_map/dot_general | solution.py:122
  204.8 0.0 all-to-all-done.1
  204.8 13.4 %convolution_convert_fusion = bf16[2048,2048]{1,0:T(8,128)(2,1)} fusion(bf16[2048,1024]{1,0:T(8,128)(2,1)} %bitcast.5, bf16[1024,1024]{1,0:T(8,128)(2,1)} %bitcast.33, bf16[1024,1024]{1,0:T(8,128)(2,1)S(1)} %bitcast.32), kind=kOutput, calls=%fused_computation.3 | convolution fusion | flops 8602517504 | bytes 16777216 | tf_op jit(solution)/shard_map/dot_general | solution.py:124
  218.2 33.6 %shard_map.73 = (bf16[2048,1024]{1,0:T(8,128)(2,1)}, f32[2048,16]{1,0:T(8,128)}) custom-call(s32[64]{0:T(128)} %copy-done.5, bf16[2048,1024]{1,0:T(8,128)(2,1)} %fusion.6.q_ref, bf16[64,32,2048]{2,1,0:T(8,128)(2,1)} %bitcast.27, bf16[64,32,2048]{2,1,0:T(8,128)(2,1)} %bitcast.28), custom_call_target="tpu_custom_call" | custom-call | flops 4294967296 | bytes 16777216 | tf_op jit(solution)/shard_map/pallas_call | solution.py:76
  251.8 77.7 %all-gather.1 = f32[8192,16]{1,0:T(8,128)} all-gather(f32[2048,16]{1,0:T(8,128)} %get-tuple-element.8), channel_id=3, replica_groups=mesh['span'=64,'head'=4] {'head'}, dimensions={0}, use_global_device_ids=true | all-gather | bytes 655360 | tf_op jit(solution)/shard_map/all_gather | solution.py:128
  329.5 2.6 reduce_max.9
  332.1 0.0 copy-start.3
  332.1 0.1 is-finite_select_fusion
  332.2 3.1 exponential_reduce_fusion
  335.2 0.0 copy-done.3
  335.3 0.3 subtract_exponential_fusion
  335.6 0.3 copy.42
  335.9 4.3 broadcast_in_dim.27
  340.2 0.0 copy-start.2
  340.2 9.4 %copy.43 = f32[2048,1024]{1,0:T(8,128)} copy(f32[2048,1024]{0,1:T(8,128)} %bitcast.29) | data formatting | bytes 16777216 | tf_op jit(solution)/shard_map/reshape | solution.py:130
  349.6 0.0 copy-done.2
  349.6 1.2 copy.44
  350.8 1.6 copy.45
  352.4 2.1 reshape.67
  354.5 9.8 %fusion = bf16[2048,1024]{1,0:T(8,128)(2,1)S(1)} fusion(bf16[1024,1024]{1,0:T(8,128)(2,1)} %reshape.67, f32[2048,1024]{1,0:T(8,128)} %copy.43, bf16[2048,1024]{1,0:T(8,128)(2,1)} %get-tuple-element.7), kind=kOutput, calls=%fused_computation.4 | convolution fusion | flops 4301258752 | bytes 18874368 | tf_op jit(solution)/shard_map/dot_general | solution.py:132
  364.3 0.0 copy-start.1
  364.3 0.4 slice.40
  364.7 3.2 concatenate.19
  367.9 0.0 reduce-scatter.2.cloned.1.call-update
  367.9 84.1 %reduce-scatter.2.cloned.1.call-done = bf16[2048,256]{1,0:T(8,128)(2,1)} async-done(((bf16[2048,1024]{1,0:T(8,128)(2,1)}), bf16[2048,256]{1,0:T(8,128)(2,1)}) %reduce-scatter.2.cloned.1.call-update) | async-done | bytes 1048592 | tf_op jit(solution)/shard_map/reduce_scatter | solution.py:134
  452.0 0.0 copy-done.1
  (5 shorter events, 0.0 us)
Async XLA Ops:
  6.5 1.0 copy-start
  6.5 186.2 %all-gather.5.cloned.1.call-start = ((), (), s32[]{:S(2)}) async-start(), calls=%async_computation.4 | async-start | bytes 8519680 | tf_op jit(solution)/shard_map/all_gather | solution.py:109
  41.7 19.3 %copy-start.5 = (s32[64]{0:T(128)}, s32[64]{0:T(128)S(1)}, u32[]{:S(2)}) copy-start(s32[64]{0:T(128)S(1)} %reshape_squeeze.3.ids) | copy-start | bytes 772
  61.1 143.7 %all-to-all-start.1 = ((bf16[64,32,1024]{2,1,0:T(8,128)(2,1)}), bf16[64,32,1024]{2,1,0:T(8,128)(2,1)}, u32[]{:S(2)}, u32[]{:S(2)}) async-start(bf16[64,32,1024]{2,1,0:T(8,128)(2,1)} %gather_fusion), calls=%async_computation.1 | async-start | bytes 8388608 | tf_op jit(solution)/shard_map/all_to_all | solution.py:112
  70.3 381.8 %reduce-scatter.2.cloned.1.call-start = ((), (), s32[]{:S(2)}) async-start(), calls=%async_computation.3 | async-start | bytes 5242880 | tf_op jit(solution)/shard_map/reduce_scatter | solution.py:134
  192.8 6.0 %copy-start.4 = (bf16[1985,1024]{1,0:T(8,128)(2,1)S(1)}, bf16[1985,1024]{1,0:T(8,128)(2,1)}, u32[]{:S(2)}) copy-start(bf16[1985,1024]{1,0:T(8,128)(2,1)} %slice.25) | copy-start | bytes 12195844
  332.1 3.2 copy-start.3
  340.2 9.4 %copy-start.2 = (bf16[64,16,1024]{2,1,0:T(8,128)(2,1)S(1)}, bf16[64,16,1024]{2,1,0:T(8,128)(2,1)}, u32[]{:S(2)}) copy-start(bf16[64,16,1024]{2,1,0:T(8,128)(2,1)} %get-tuple-element.10) | copy-start | bytes 6291460
  364.3 87.8 %copy-start.1 = (bf16[1024,256]{1,0:T(8,128)(2,1)S(1)}, bf16[1024,256]{1,0:T(8,128)(2,1)}, u32[]{:S(2)}) copy-start(bf16[1024,256]{1,0:T(8,128)(2,1)} %param.10) | copy-start | bytes 1572868
Sparse Core Ops, SparseCore 0:
  40.9 151.8 all-gather.4
  368.0 83.9 reduce-scatter.1

commit v2 on v1

v2 whole, which is shorter than its diff:
```python
import jax
import jax.numpy as jnp
from jax import lax
from jax.experimental import pallas as pl
from jax.experimental.pallas import tpu as pltpu
from jax.sharding import PartitionSpec as P

HEAD_DIM = 64
SPAN_LEN = 64
SEQ_LEN = 2048
D = 1024
HEADS = 16
SPANS = 32
OFFSET = SPAN_LEN - 1
GROUP = 256
F32 = jnp.float32
BF16 = jnp.bfloat16


def head_mask(rows, cols):
    r = lax.broadcasted_iota(jnp.int32, (rows, cols), 0) // HEAD_DIM
    c = lax.broadcasted_iota(jnp.int32, (rows, cols), 1) // HEAD_DIM
    return r == c


MESH = pl.DeviceIdType.MESH
BLK = 128
NB = SEQ_LEN // BLK


def attention_block(b, ids, q_ref, kv_ref, ctx, lse_own):
    mask = head_mask(GROUP, GROUP)
    ones = jnp.where(mask, 1.0, 0.0).astype(BF16)
    zero = jnp.zeros((GROUP, GROUP), BF16)
    lane = lax.broadcasted_iota(jnp.int32, (SPAN_LEN, 128), 1)
    low = lane < HEAD_DIM
    stats = []
    for sp in range(BLK // SPAN_LEN):
        j = b * (BLK // SPAN_LEN) + sp
        first = ids[2 * j]
        second = ids[2 * j + 1]
        rows = pl.ds(pl.multiple_of(j * SPAN_LEN, SPAN_LEN), SPAN_LEN)
        lses = jnp.zeros((SPAN_LEN, 128), F32)
        for g in range(D // GROUP):
            cols = slice(g * GROUP, (g + 1) * GROUP)
            vcols = slice(D + g * GROUP, D + (g + 1) * GROUP)
            k4 = jnp.concatenate([kv_ref[first, :, cols], kv_ref[second, :, cols]], axis=0)
            v4 = jnp.concatenate([kv_ref[first, :, vcols], kv_ref[second, :, vcols]], axis=0)
            kbd = jnp.where(mask, jnp.concatenate([k4] * 4, axis=0), zero)
            vbd = jnp.where(mask, jnp.concatenate([v4] * 4, axis=0), zero)
            s = lax.dot_general(
                q_ref[rows, cols], kbd, (((1,), (1,)), ((), ())), preferred_element_type=F32
            ) * (HEAD_DIM ** -0.5)
            tops = []
            for half in range(2):
                part = s[:, half * 128 : (half + 1) * 128]
                m0 = jnp.max(jnp.where(low, part, -jnp.inf), axis=1, keepdims=True)
                m1 = jnp.max(jnp.where(low, -jnp.inf, part), axis=1, keepdims=True)
                tops.append(jnp.where(low, m0, m1))
            top = jnp.concatenate(tops, axis=1)
            p = jnp.exp(s - top).astype(BF16)
            total = jnp.dot(p, ones, preferred_element_type=F32)
            c = jnp.dot(p, vbd, preferred_element_type=F32)
            ctx[b, sp * SPAN_LEN : (sp + 1) * SPAN_LEN, cols] = (c / total).astype(BF16)
            lse = top + jnp.log(total)
            for n in range(4):
                lses = jnp.where(lane == g * 4 + n, lse[:, n * 64 : n * 64 + 1], lses)
        stats.append(lses)
    lse_own[b] = jnp.concatenate(stats, axis=0).T[:HEADS]


def combine_kernel(
    ids, q_ref, kv_ref, o_ref, out_ref,
    ctx, lse_own, lse_in, opp, opp_in, side, own, sendb, sum_in,
    lse_send, lse_recv, opp_send, opp_recv, sum_send, sum_recv,
):
    h = lax.axis_index("head")
    peers = [(h + d) % 4 for d in range(4)]
    toward = (peers[1], peers[3])
    barrier = pltpu.get_barrier_semaphore()
    for d in range(1, 4):
        pl.semaphore_signal(barrier, inc=1, device_id={"head": peers[d]}, device_id_type=MESH)
    pl.semaphore_wait(barrier, 3)

    def lse_copy(d, b):
        return pltpu.make_async_remote_copy(
            src_ref=lse_own.at[b], dst_ref=lse_in.at[d - 1, b],
            send_sem=lse_send.at[d - 1], recv_sem=lse_recv.at[d - 1, b],
            device_id={"head": peers[d]}, device_id_type=MESH,
        )

    def opp_copy(w, b):
        return pltpu.make_async_remote_copy(
            src_ref=opp.at[w, b], dst_ref=opp_in.at[w, b],
            send_sem=opp_send.at[w], recv_sem=opp_recv.at[w, b],
            device_id={"head": toward[w]}, device_id_type=MESH,
        )

    def sum_copy(w, b):
        return pltpu.make_async_remote_copy(
            src_ref=sendb.at[w, b], dst_ref=sum_in.at[w, b],
            send_sem=sum_send.at[w], recv_sem=sum_recv.at[w, b],
            device_id={"head": toward[w]}, device_id_type=MESH,
        )

    row = lax.broadcasted_iota(jnp.int32, (2 * HEADS, D), 0) % HEADS
    col = lax.broadcasted_iota(jnp.int32, (2 * HEADS, D), 1) // HEAD_DIM
    expand = jnp.where(row == col, 1.0, 0.0).astype(BF16)

    def finish(b):
        for w in range(2):
            sum_copy(w, b).wait_recv()
        rows = pl.ds(pl.multiple_of(b * BLK, BLK), BLK)
        total = own[b] + (sum_in[0, b].astype(F32) + sum_in[1, b].astype(F32))
        out_ref[rows, :] = total.astype(BF16)

    def forward(b):
        half = BLK // 2
        for w in range(2):
            opp_copy(w, b).wait_recv()
            part = opp_in[w, b].astype(F32)
            if w == 0:
                top, low = side[w, b, :half] + part, side[w, b, half:]
            else:
                top, low = side[w, b, :half], side[w, b, half:] + part
            sendb[w, b, :half] = top.astype(BF16)
            sendb[w, b, half:] = low.astype(BF16)
            sum_copy(w, b).start()

    def project(b):
        for d in range(1, 4):
            lse_copy(d, b).wait_recv()
        mine = lse_own[b]
        others = [lse_in[d, b] for d in range(3)]
        top = jnp.maximum(jnp.maximum(mine, others[0]), jnp.maximum(others[1], others[2]))
        part = jnp.exp(mine - top)
        total = part
        for other in others:
            total = total + jnp.exp(other - top)
        share = part / total
        high = share.astype(BF16).astype(F32)
        both = jnp.concatenate([high, share - high], axis=0).T.astype(BF16)
        wide = jnp.dot(both, expand, preferred_element_type=F32)
        scaled = (ctx[b].astype(F32) * wide).astype(BF16)
        far = jnp.dot(scaled, o_ref[peers[2]], preferred_element_type=F32).astype(BF16)
        for w in range(2):
            opp[w, b] = far[w * (BLK // 2) : (w + 1) * (BLK // 2)]
        side[0, b] = jnp.dot(scaled, o_ref[peers[1]], preferred_element_type=F32)
        for w in range(2):
            opp_copy(w, b).start()
        side[1, b] = jnp.dot(scaled, o_ref[peers[3]], preferred_element_type=F32)
        own[b] = jnp.dot(scaled, o_ref[h], preferred_element_type=F32)

    def attend(b):
        attention_block(b, ids, q_ref, kv_ref, ctx, lse_own)
        for d in range(1, 4):
            lse_copy(d, b).start()

    stages = ((finish, 6), (forward, 4), (project, 2), (attend, 0))

    def step(i, carry):
        for stage, lag in stages:
            b = i - lag

            @pl.when(jnp.logical_and(b >= 0, b < NB))
            def _():
                stage(b)

        return carry

    lax.fori_loop(0, NB + 6, step, 0)

    def drain(ref, sem):
        pltpu.make_async_copy(ref, ref, sem).wait()

    for d in range(3):
        drain(lse_own, lse_send.at[d])
    for w in range(2):
        drain(opp.at[w], opp_send.at[w])
        drain(sendb.at[w], sum_send.at[w])


def combine(ids, queries, projected, columns):
    vmem = pl.BlockSpec(memory_space=pltpu.VMEM)
    return pl.pallas_call(
        combine_kernel,
        out_shape=jax.ShapeDtypeStruct((SEQ_LEN, 256), BF16),
        in_specs=[pl.BlockSpec(memory_space=pltpu.SMEM), vmem, vmem, vmem],
        out_specs=vmem,
        scratch_shapes=[
            pltpu.VMEM((NB, BLK, D), BF16),
            pltpu.VMEM((NB, HEADS, BLK), F32),
            pltpu.VMEM((3, NB, HEADS, BLK), F32),
            pltpu.VMEM((2, NB, BLK // 2, 256), BF16),
            pltpu.VMEM((2, NB, BLK // 2, 256), BF16),
            pltpu.VMEM((2, NB, BLK, 256), F32),
            pltpu.VMEM((NB, BLK, 256), F32),
            pltpu.VMEM((2, NB, BLK, 256), BF16),
            pltpu.VMEM((2, NB, BLK, 256), BF16),
            pltpu.SemaphoreType.DMA((3,)),
            pltpu.SemaphoreType.DMA((3, NB)),
            pltpu.SemaphoreType.DMA((2,)),
            pltpu.SemaphoreType.DMA((2, NB)),
            pltpu.SemaphoreType.DMA((2,)),
            pltpu.SemaphoreType.DMA((2, NB)),
        ],
        compiler_params=pltpu.CompilerParams(
            collective_id=1, has_side_effects=True, vmem_limit_bytes=60 << 20
        ),
        cost_estimate=pl.CostEstimate(
            flops=60_000_000_000, bytes_accessed=16 << 20, transcendentals=1 << 21
        ),
        name="combine",
    )(ids, queries, projected, columns)


def body(
    decoder_states, encodings, neighbor_table, query_weight, key_weight, value_weight, out_weight
):
    s = lax.axis_index("span")
    h = lax.axis_index("head")
    shard_ids = neighbor_table[:, :, 0].reshape(-1)
    slot_ids = neighbor_table[:, :, 1].reshape(-1)
    numbering = jnp.arange(64, dtype=jnp.int32)
    placed = shard_ids[None, :] == numbering[:, None]
    request = jnp.sum(jnp.where(placed, slot_ids[None, :], 0), axis=1)
    wanted = lax.all_to_all(request, "span", split_axis=0, concat_axis=0, tiled=True)

    column_pieces = [
        lax.dynamic_slice_in_dim(w, s * 16, 16, 0)
        for w in (query_weight, key_weight, value_weight)
    ]
    small = lax.all_gather(jnp.concatenate(column_pieces, axis=0), "head", axis=1, tiled=True)
    out_piece = lax.dynamic_slice_in_dim(out_weight, s * 4, 4, 0)
    out_small = lax.all_gather(out_piece, "head", axis=0, tiled=True)
    pieces = jnp.concatenate([small, out_small], axis=0)
    whole = lax.all_gather(pieces, "span", axis=0)

    selected = encodings[wanted]
    arrived = lax.all_to_all(selected, "span", split_axis=0, concat_axis=0, tiled=True)

    whole_q = whole[:, 0:16].reshape(D, D)
    whole_k = whole[:, 16:32].reshape(D, D)
    whole_v = whole[:, 32:48].reshape(D, D)
    whole_o = whole[:, 48:64].reshape(64, 4, 4, D).transpose(1, 0, 2, 3).reshape(D, D)

    shifted = jnp.concatenate(
        [decoder_states[OFFSET:], jnp.zeros((OFFSET, D), BF16)], axis=0
    )
    queries = jnp.dot(shifted, whole_q, preferred_element_type=F32).astype(BF16)
    both = jnp.concatenate([whole_k, whole_v], axis=1)
    projected = jnp.dot(
        arrived.reshape(-1, D), both, preferred_element_type=F32
    ).astype(BF16).reshape(64, 32, 2 * D)
    columns = whole_o.reshape(D, 4, 256).transpose(1, 0, 2)
    summed = combine(shard_ids, queries, projected, columns)
    return jnp.concatenate([jnp.zeros((OFFSET, 256), BF16), summed[: SEQ_LEN - OFFSET]], axis=0)


def solution(mesh):
    return jax.shard_map(
        body,
        mesh=mesh,
        in_specs=(
            P("span", None),
            P("span", "head", None),
            P("span", None, None),
            P(None, "head"),
            P(None, "head"),
            P(None, "head"),
            P("head", None),
        ),
        out_specs=P("span", "head"),
        check_vma=False,
    )
```

time: 461 us -> 344 us (0.75)
  waiting for transfers between devices: 201 us -> 117 us
  blocking collectives: 121 us -> 43.7 us
  Pallas kernels: 33.6 us -> 101 us
  local copies, waits for them, and re-layouts: 42.6 us -> 30.7 us
  matrix products: 29.2 us -> 21 us
  other arithmetic: 8.1 us -> 2.01 us
    reduce_scatter x1 -> x0, waiting for transfers between devices: 84.1 us -> none  [body(): return lax.psum_scatter(partial, 'head', scatter_dimension=1, tiled=True)]
    all_gather x1 -> x0, blocking collectives: 77.7 us -> none  [body(): all_lse = lax.all_gather(lse, 'head', axis=0)]
    pallas_call x1, Pallas kernels: 33.6 us -> 101 us  [combine(): pl.pallas_call(combine_kernel, out_shape=jax.ShapeDtypeStruct((SEQ_LEN, 2...]
    reshape x2 -> x0, local copies, waits for them, and re-layouts: 11.5 us -> none  [the longest x1 9.42 us: body(): share = jnp.repeat(share, HEAD_DIM, axis=1)]
    dot_general x1 -> x0, matrix products: 9.78 us -> none  [body(): partial = jnp.dot(scaled, whole_o, preferred_element_type=F32).astype(BF16)]
    slice x1 -> x2, local copies, waits for them, and re-layouts: 1.15 us -> 6.95 us  [body(): whole[:, 48:64].reshape(64, 4, 4, D).transpose(1, 0, 2, 3).reshape(D, D)]
    another operation x0 -> x2, local copies, waits for them, and re-layouts: none -> 5.6 us  [body(): columns = whole_o.reshape(D, 4, 256).transpose(1, 0, 2)]
    slice x2 -> x1, local copies, waits for them, and re-layouts: 5.97 us -> 1.28 us  [body(): summed[:SEQ_LEN - OFFSET]]
  transfers between devices with their start and end apart: 3 -> 2, of which waited for: 2 -> 1; matrix products, arithmetic and copies ran while one was open for 5% -> 10% of each run, Pallas kernels for 0% -> 0%
where the time goes in v2:
time: 344 us; the launch traced here: 339 us
  waiting for transfers between devices  117 us (34%)
  Pallas kernels  101 us (29%)
  blocking collectives  43.7 us (13%)
  local copies, waits for them, and re-layouts  30.7 us (9%)
  matrix products  21 us (6%)
  between operations  13.5 us (4%)
  starting transfers between devices  9.21 us (3%)
    all_gather x1, waiting for transfers between devices, body(): whole = lax.all_gather(pieces, 'span', axis=0)  117 us
    pallas_call x1, Pallas kernels, combine(): pl.pallas_call(combine_kernel, out_shape=jax.ShapeDtypeStruct((SEQ_LEN, 2...  101 us
    all_gather x1, blocking collectives, body(): lax.all_gather(jnp.concatenate(column_pieces, axis=0), 'head', axis=1, ti...  17.3 us
    all_gather x1, blocking collectives, body(): out_small = lax.all_gather(out_piece, 'head', axis=0, tiled=True)  13.7 us
    dot_general x1, matrix products, body(): jnp.dot(arrived.reshape(-1, D), both, preferred_element_type=F32)  13.2 us
    all_to_all x1, blocking collectives, body(): lax.all_to_all(request, 'span', split_axis=0, concat_axis=0, tiled=True)  12.6 us
    all_to_all x1, starting transfers between devices, body(): lax.all_to_all(selected, 'span', split_axis=0, concat_axis=0, tiled=True)  9.21 us
    dot_general x1, matrix products, body(): queries = jnp.dot(shifted, whole_q, preferred_element_type=F32).astype(BF16)  7.75 us
  transfers between devices with their start and end apart: 2, of which 1 were waited for; matrix products, arithmetic and copies ran while one was open for 10% of the time, Pallas kernels for 0%

profile of v2, /device:TPU:20, one launch (start us, length us, event | category | flops | bytes accessed | tf_op | source)
XLA Modules:
  0.0 338.6 jit_solution(4775369263688182055)
XLA Ops:
  6.5 0.0 copy-start
  6.5 0.0 all-gather.4.cloned.1.call-start
  6.5 1.0 copy-done
  7.6 0.7 constant_dynamic-slice_fusion
  8.3 17.3 %all_gather.12 = bf16[48,1024]{1,0:T(8,128)(2,1)S(1)} all-gather(bf16[48,256]{1,0:T(8,128)(2,1)S(1)} %pad_maximum_fusion.1), channel_id=1, replica_groups=mesh['span'=64,'head'=4] {'head'}, dimensions={1}, use_global_device_ids=true | all-gather | bytes 122880 | tf_op jit(solution)/shard_map/all_gather | solution.py:233
  25.6 0.7 dynamic-slice_bitcast_fusion
  26.4 13.7 %all-gather.1 = bf16[4,4,1024]{2,1,0:T(4,128)(2,1)S(1)} all-gather(bf16[1,4,1024]{2,1,0:T(4,128)(2,1)S(1)} %dynamic-slice_bitcast_fusion), channel_id=1, replica_groups=mesh['span'=64,'head'=4] {'head'}, dimensions={0}, use_global_device_ids=true | all-gather | bytes 40960 | tf_op jit(solution)/shard_map/all_gather | solution.py:235
  40.1 0.7 pad_maximum_fusion
  40.8 0.0 all-gather.4.cloned.1.call-update
  40.8 0.8 fusion.12
  41.5 0.1 copy.34
  41.6 0.1 reshape_squeeze.3.ids
  41.7 0.0 copy-start.3
  41.7 0.1 copy.35
  41.8 0.1 broadcast_in_dim.18
  41.9 0.1 select_reduce_fusion
  42.1 0.1 copy.36
  42.2 12.6 %all_to_all.17 = s32[64,1,1]{2,1,0:T(1,128)S(1)} all-to-all(s32[64,1,1]{2,1,0:T(1,128)S(1)} %copy.36), channel_id=1, replica_groups=mesh['span'=64,'head'=4] {'span'}, dimensions={0} | all-to-all | bytes 512 | tf_op jit(solution)/shard_map/all_to_all | solution.py:227
  54.8 1.2 reduce
  56.0 5.0 %gather_fusion = bf16[64,32,1024]{2,1,0:T(8,128)(2,1)} fusion(bf16[64,32,1024]{2,1,0:T(8,128)(2,1)} %param.8, s32[1024]{0:T(1024)S(1)} %pad_clamp_fusion), kind=kCustom, calls=%fused_computation | custom fusion | bytes 8388864 | tf_op jit(solution)/shard_map/gather | solution.py:239
  61.0 0.0 copy-done.3
  61.0 9.2 %all-to-all-start.1 = ((bf16[64,32,1024]{2,1,0:T(8,128)(2,1)}), bf16[64,32,1024]{2,1,0:T(8,128)(2,1)}, u32[]{:S(2)}, u32[]{:S(2)}) async-start(bf16[64,32,1024]{2,1,0:T(8,128)(2,1)} %gather_fusion), calls=%async_computation.1 | async-start | bytes 8388608 | tf_op jit(solution)/shard_map/all_to_all | solution.py:240
  70.2 5.3 %slice.25 = bf16[1985,1024]{1,0:T(8,128)(2,1)} slice(bf16[2048,1024]{1,0:T(8,128)(2,1)} %param.7), slice={[63:2048], [0:1024]} | slice | bytes 8130560 | tf_op jit(solution)/shard_map/slice | solution.py:248
  75.5 117.3 %all-gather.4.cloned.1.call-done = bf16[4096,1024]{1,0:T(8,128)(2,1)} async-done(((bf16[64,1024]{1,0:T(8,128)(2,1)}), bf16[4096,1024]{1,0:T(8,128)(2,1)}) %all-gather.4.cloned.1.call-update) | async-done | bytes 8388624 | tf_op jit(solution)/shard_map/all_gather | solution.py:237
  192.8 5.8 %fusion.11 = (bf16[64,16,1024]{2,1,0:T(8,128)(2,1)S(1)}, bf16[64,16,1024]{2,1,0:T(8,128)(2,1)}, bf16[64,16,1024]{2,1,0:T(8,128)(2,1)}, bf16[64,16,1024]{2,1,0:T(8,128)(2,1)}) fusion(bf16[64,64,1024]{2,1,0:T(8,128)(2,1)} %bitcast.25), kind=kLoop, calls=%fused_computation.22 | loop fusion | bytes 16777216 | tf_op jit(solution)/shard_map/slice | solution.py:245
  198.6 1.2 copy.37
  199.7 1.6 copy.38
  201.3 2.2 reshape_reshape.3
  203.6 0.0 copy-start.1
  203.6 3.4 copy.41
  206.9 0.0 copy-done.1
  206.9 0.0 copy-start.2
  206.9 7.7 %fusion.5.q_ref = bf16[2048,1024]{1,0:T(8,128)(2,1)} fusion(bf16[1024,1024]{1,0:T(8,128)(2,1)} %bitcast.30, bf16[1985,1024]{1,0:T(8,128)(2,1)S(1)} %copy-done.1), kind=kOutput, calls=%fused_computation.7 | convolution fusion | flops 4297064448 | bytes 10356736 | tf_op jit(solution)/shard_map/dot_general | solution.py:250
  214.7 0.0 all-to-all-done.1
  214.7 0.0 copy-done.2
  214.7 13.2 %convolution_convert_fusion = bf16[2048,2048]{1,0:T(8,128)(2,1)} fusion(bf16[2048,1024]{1,0:T(8,128)(2,1)} %bitcast.5, bf16[1024,1024]{1,0:T(8,128)(2,1)S(1)} %bitcast.28, bf16[1024,1024]{1,0:T(8,128)(2,1)} %bitcast.29), kind=kOutput, calls=%fused_computation.1 | convolution fusion | flops 8602517504 | bytes 16777216 | tf_op jit(solution)/shard_map/dot_general | solution.py:252
  227.9 101.3 %combine.1 = bf16[2048,256]{1,0:T(8,128)(2,1)} custom-call(s32[64]{0:T(128)} %copy-done.3, bf16[2048,1024]{1,0:T(8,128)(2,1)} %fusion.5.q_ref, bf16[64,32,2048]{2,1,0:T(8,128)(2,1)} %bitcast.32, bf16[4,1024,256]{2,1,0:T(8,128)(2,1)} %bitcast.27), custom_call_target="tpu_custom_call" | custom-call | flops 60000002048 | bytes 16777216 | tf_op jit(solution)/shard_map/combine/pallas_call | solution.py:185
  329.2 1.3 slice.31
  330.5 1.2 concatenate.19
  (5 shorter events, 0.0 us)
Async XLA Ops:
  6.5 1.0 copy-start
  6.5 186.2 %all-gather.4.cloned.1.call-start = ((), (), s32[]{:S(2)}) async-start(), calls=%async_computation.2 | async-start | bytes 8519680 | tf_op jit(solution)/shard_map/all_gather | solution.py:237
  41.7 19.3 %copy-start.3 = (s32[64]{0:T(128)}, s32[64]{0:T(128)S(1)}, u32[]{:S(2)}) copy-start(s32[64]{0:T(128)S(1)} %reshape_squeeze.3.ids) | copy-start | bytes 772
  61.0 153.7 %all-to-all-start.1 = ((bf16[64,32,1024]{2,1,0:T(8,128)(2,1)}), bf16[64,32,1024]{2,1,0:T(8,128)(2,1)}, u32[]{:S(2)}, u32[]{:S(2)}) async-start(bf16[64,32,1024]{2,1,0:T(8,128)(2,1)} %gather_fusion), calls=%async_computation.1 | async-start | bytes 8388608 | tf_op jit(solution)/shard_map/all_to_all | solution.py:240
  203.6 3.4 copy-start.1
  206.9 7.8 %copy-start.2 = (bf16[64,16,1024]{2,1,0:T(8,128)(2,1)S(1)}, bf16[64,16,1024]{2,1,0:T(8,128)(2,1)}, u32[]{:S(2)}) copy-start(bf16[64,16,1024]{2,1,0:T(8,128)(2,1)} %get-tuple-element.6) | copy-start | bytes 6291460
Sparse Core Ops, SparseCore 0:
  40.9 151.8 all-gather.3

commit v3 on v2

v3 whole, which is shorter than its diff:
```python
import functools

import jax
import jax.numpy as jnp
from jax import lax
from jax.experimental import pallas as pl
from jax.experimental.pallas import tpu as pltpu
from jax.sharding import PartitionSpec as P

HEAD_DIM = 64
SPAN_LEN = 64
SEQ_LEN = 2048
D = 1024
HEADS = 16
SPANS = 32
SHARDS = 64
NTOK_PART = 32
OFFSET = SPAN_LEN - 1
GROUP = 256
BLK = 128
NB = SEQ_LEN // BLK
QT = 256
F32 = jnp.float32
BF16 = jnp.bfloat16
MESH = pl.DeviceIdType.MESH


def far(o):
    return min(o[0], 4 - o[0]) + min(o[1], 4 - o[1]) + o[2]


OFFSETS = [(0, 0, 0, 0)] + sorted(
    [
        (oy, ox, oz, oc)
        for oy in range(4)
        for ox in range(4)
        for oz in range(2)
        for oc in range(2)
        if (oy, ox, oz, oc) != (0, 0, 0, 0)
    ],
    key=lambda o: -far(o),
)


def head_mask(rows, cols):
    r = lax.broadcasted_iota(jnp.int32, (rows, cols), 0) // HEAD_DIM
    c = lax.broadcasted_iota(jnp.int32, (rows, cols), 1) // HEAD_DIM
    return r == c


def attention_block(b, place, q, kv, ctx, lse_own):
    mask = head_mask(GROUP, GROUP)
    ones = jnp.where(mask, 1.0, 0.0).astype(BF16)
    zero = jnp.zeros((GROUP, GROUP), BF16)
    lane = lax.broadcasted_iota(jnp.int32, (SPAN_LEN, 128), 1)
    low = lane < HEAD_DIM
    stats = []
    for sp in range(BLK // SPAN_LEN):
        j = b * (BLK // SPAN_LEN) + sp
        first = place[2 * j]
        second = place[2 * j + 1]
        rows = pl.ds(pl.multiple_of(j * SPAN_LEN, SPAN_LEN), SPAN_LEN)
        lses = jnp.zeros((SPAN_LEN, 128), F32)
        for g in range(D // GROUP):
            cols = slice(g * GROUP, (g + 1) * GROUP)
            k4 = jnp.concatenate([kv[g, first], kv[g, second]], axis=0)
            v4 = jnp.concatenate([kv[4 + g, first], kv[4 + g, second]], axis=0)
            kbd = jnp.where(mask, jnp.concatenate([k4] * 4, axis=0), zero)
            vbd = jnp.where(mask, jnp.concatenate([v4] * 4, axis=0), zero)
            s = lax.dot_general(
                q[rows, cols], kbd, (((1,), (1,)), ((), ())), preferred_element_type=F32
            ) * (HEAD_DIM ** -0.5)
            tops = []
            for half in range(2):
                part = s[:, half * 128 : (half + 1) * 128]
                m0 = jnp.max(jnp.where(low, part, -jnp.inf), axis=1, keepdims=True)
                m1 = jnp.max(jnp.where(low, -jnp.inf, part), axis=1, keepdims=True)
                tops.append(jnp.where(low, m0, m1))
            top = jnp.concatenate(tops, axis=1)
            p = jnp.exp(s - top).astype(BF16)
            total = jnp.dot(p, ones, preferred_element_type=F32)
            c = jnp.dot(p, vbd, preferred_element_type=F32)
            ctx[b, sp * SPAN_LEN : (sp + 1) * SPAN_LEN, cols] = (c / total).astype(BF16)
            lse = top + jnp.log(total)
            for n in range(4):
                lses = jnp.where(lane == g * 4 + n, lse[:, n * 64 : n * 64 + 1], lses)
        stats.append(lses)
    lse_own[b] = jnp.concatenate(stats, axis=0).T[:HEADS]


def kernel(
    place, req, enc_hbm, dec_hbm, wq, wk, wv, wo, out,
    enc, dec, want, want_s, stage, arr, w, q, carry, kv,
    ctx, lse_own, lse_in, opp, opp_in, side, own, sendb, sum_in,
    load_sem, req_send, req_recv, arr_send, arr_recv,
    z_send, z_recv, a_send, a_recv, one_send, one_recv, two_send, two_recv, c_send, c_recv,
    lse_send, lse_recv, opp_send, opp_recv, sum_send, sum_recv,
):
    h = lax.axis_index("head")
    s = lax.axis_index("span")
    core = s % 2
    zl = (s // 2) % 2
    x = (s // 4) % 4
    y = s // 16
    peers = [(h + d) % 4 for d in range(4)]
    toward = (peers[1], peers[3])

    def index(yy, xx, zz, cc):
        return ((yy * 4 + xx) * 2 + zz) * 2 + cc

    def target(o):
        return index((y + o[0]) % 4, (x + o[1]) % 4, (zl + o[2]) % 2, (core + o[3]) % 2)

    def send(src, dst, send_sem, recv_sem, to):
        return pltpu.make_async_remote_copy(
            src_ref=src, dst_ref=dst, send_sem=send_sem, recv_sem=recv_sem,
            device_id=to, device_id_type=MESH,
        )

    loads = [
        pltpu.make_async_copy(src, w.at[h, i], load_sem.at[i])
        for i, src in enumerate((wq, wk, wv))
    ] + [
        pltpu.make_async_copy(
            wo.at[:, :, :, k * 256 : (k + 1) * 256],
            w.at[h, 3, k // 2, 2 * (k % 2) : 2 * (k % 2) + 2],
            load_sem.at[3 + k],
        )
        for k in range(4)
    ]
    enc_load = pltpu.make_async_copy(enc_hbm, enc, load_sem.at[7])
    dec_load = pltpu.make_async_copy(dec_hbm, dec.at[pl.ds(0, SEQ_LEN)], load_sem.at[8])
    for load in loads:
        load.start()
    enc_load.start()
    dec_load.start()

    barrier = pltpu.get_barrier_semaphore()
    for o in OFFSETS[1:]:
        pl.semaphore_signal(barrier, inc=1, device_id={"span": target(o)}, device_id_type=MESH)
    for d in range(1, 4):
        pl.semaphore_signal(barrier, inc=1, device_id={"head": peers[d]}, device_id_type=MESH)
    want[s] = req[s]
    dec[SEQ_LEN:] = jnp.zeros((SPAN_LEN, D), BF16)
    pl.semaphore_wait(barrier, SHARDS - 1 + 3)

    for o in OFFSETS[1:]:
        t = target(o)
        send(req.at[t], want.at[s], req_send, req_recv, {"span": t}).start()

    def z_copy(d):
        piece = w.at[h, :, core, y, x, pl.ds(pl.multiple_of(zl * 16, 16), 16), :]
        return send(piece, piece, z_send.at[d - 1], z_recv.at[d - 1], {"head": peers[d]})

    def a_copy(d):
        piece = w.at[peers[d], :, core, y, x, pl.ds(pl.multiple_of(zl * 16, 16), 16), :]
        to = {"span": index(y, x, 1 - zl, core)}
        return send(piece, piece, a_send.at[d - 1], a_recv.at[d - 1], to)

    def one_copy(half, e, d):
        piece = w.at[peers[d], 2 * half : 2 * half + 2, core, y, x]
        to = index(y, (x + e) % 4, zl, core) if half == 0 else index((y + e) % 4, x, zl, core)
        n = (half * 3 + e - 1) * 3 + d - 1
        return send(piece, piece, one_send.at[n], one_recv.at[n], {"span": to})

    def two_copy(half, e, d):
        if half == 0:
            piece = w.at[peers[d], 0:2, core, y]
            to = index((y + e) % 4, x, zl, core)
        else:
            piece = w.at[peers[d], 2:4, core, :, x]
            to = index(y, (x + e) % 4, zl, core)
        n = (half * 3 + e - 1) * 3 + d - 1
        return send(piece, piece, two_send.at[n], two_recv.at[n], {"span": to})

    def c_copy(d):
        piece = w.at[peers[d], :, core]
        return send(piece, piece, c_send.at[d - 1], c_recv.at[d - 1], {"span": index(y, x, zl, 1 - core)})

    ring = [(half, e, d) for e in (1, 2, 3) for d in (1, 2, 3) for half in (0, 1)]
    weight_copies = [z_copy(d) for d in (1, 2, 3)] + [a_copy(d) for d in (1, 2, 3)]
    weight_copies += [one_copy(*r) for r in ring] + [two_copy(*r) for r in ring]
    weight_copies += [c_copy(d) for d in (1, 2, 3)]

    def arr_copy(i):
        to = {"span": target(OFFSETS[i])}
        return send(stage.at[i], arr.at[i], arr_send, arr_recv.at[i], to)

    def issue(lo, hi):
        for i in range(lo, hi):
            stage[i] = enc[want_s[target(OFFSETS[i]), 0, 0]]
            if i > 1:
                arr_copy(i - 1).start()

    for load in loads:
        load.wait()
    for d in (1, 2, 3):
        z_copy(d).start()
    everyone = pltpu.make_async_copy(
        want.at[pl.ds(0, SHARDS - 1)], want.at[pl.ds(0, SHARDS - 1)], req_recv
    )
    everyone.wait()
    to_scalar = pltpu.make_async_copy(want, want_s, load_sem.at[9])
    to_scalar.start()
    enc_load.wait()
    to_scalar.wait()
    issue(1, 5)
    for d in (1, 2, 3):
        z_copy(d).wait_recv()
    for d in (1, 2, 3):
        a_copy(d).start()
    issue(5, 9)
    for d in (1, 2, 3):
        a_copy(d).wait_recv()
    for r in ring:
        one_copy(*r).start()
    issue(9, 17)
    for r in ring:
        one_copy(*r).wait_recv()
    for r in ring:
        two_copy(*r).start()
    issue(17, SHARDS)
    arr[0] = enc[want_s[s, 0, 0]]
    arr_copy(SHARDS - 1).start()
    for r in ring:
        two_copy(*r).wait_recv()
    for d in (1, 2, 3):
        c_copy(d).start()
    dec_load.wait()
    for d in (1, 2, 3):
        c_copy(d).wait_recv()

    def weight(group, i):
        return w[group, i].reshape(D, GROUP)

    for g in range(4):
        head_rows = jnp.dot(dec[48:64], weight(g, 0), preferred_element_type=F32)
        carry[:, g * GROUP : (g + 1) * GROUP] = head_rows[8:16]

    first_row = lax.broadcasted_iota(jnp.int32, (QT, GROUP), 0) == 0

    def query_tile(t, state):
        source = dec[pl.ds(pl.multiple_of(t * QT + 64, 64), QT)]
        for g in range(4):
            cols = slice(g * GROUP, (g + 1) * GROUP)
            tile = jnp.dot(source, weight(g, 0), preferred_element_type=F32)
            before = carry[7:8, cols]
            moved = jnp.where(first_row, before, pltpu.roll(tile, 1, 0))
            q[pl.ds(pl.multiple_of(t * QT, QT), QT), cols] = moved.astype(BF16)
            carry[:, cols] = tile[QT - 8 :]
        return state

    lax.fori_loop(0, SEQ_LEN // QT, query_tile, 0)

    def project_chunk(k, state):
        for i in range(8):
            n = 8 * k + i

            @pl.when(n > 0)
            def _():
                send(stage.at[n], arr.at[n], arr_send, arr_recv.at[n], {"span": s}).wait_recv()

        tokens = arr[pl.ds(8 * k, 8)].reshape(8 * NTOK_PART, D)

        def columns(n, inner):
            part = jnp.dot(tokens, weight(n % 4, 1 + n // 4), preferred_element_type=F32)
            kv[n, pl.ds(8 * k, 8)] = part.astype(BF16).reshape(8, NTOK_PART, GROUP)
            return inner

        return lax.fori_loop(0, 8, columns, state)

    lax.fori_loop(0, SHARDS // 8, project_chunk, 0)

    def lse_copy(d, b):
        return send(
            lse_own.at[b], lse_in.at[d - 1, b], lse_send.at[d - 1], lse_recv.at[d - 1, b],
            {"head": peers[d]},
        )

    def opp_copy(way, b):
        return send(
            opp.at[way, b], opp_in.at[way, b], opp_send.at[way], opp_recv.at[way, b],
            {"head": toward[way]},
        )

    def sum_copy(way, b):
        return send(
            sendb.at[way, b], sum_in.at[way, b], sum_send.at[way], sum_recv.at[way, b],
            {"head": toward[way]},
        )

    row = lax.broadcasted_iota(jnp.int32, (2 * HEADS, D), 0) % HEADS
    col = lax.broadcasted_iota(jnp.int32, (2 * HEADS, D), 1) // HEAD_DIM
    expand = jnp.where(row == col, 1.0, 0.0).astype(BF16)

    def finish(b):
        for way in range(2):
            sum_copy(way, b).wait_recv()
        rows = pl.ds(pl.multiple_of(b * BLK, BLK), BLK)
        total = own[b] + (sum_in[0, b].astype(F32) + sum_in[1, b].astype(F32))
        out[rows, :] = total.astype(BF16)

    def forward(b):
        half = BLK // 2
        for way in range(2):
            opp_copy(way, b).wait_recv()
            part = opp_in[way, b].astype(F32)
            if way == 0:
                upper, lower = side[way, b, :half] + part, side[way, b, half:]
            else:
                upper, lower = side[way, b, :half], side[way, b, half:] + part
            sendb[way, b, :half] = upper.astype(BF16)
            sendb[way, b, half:] = lower.astype(BF16)
            sum_copy(way, b).start()

    def project(b):
        for d in range(1, 4):
            lse_copy(d, b).wait_recv()
        mine = lse_own[b]
        others = [lse_in[d, b] for d in range(3)]
        top = jnp.maximum(jnp.maximum(mine, others[0]), jnp.maximum(others[1], others[2]))
        part = jnp.exp(mine - top)
        total = part
        for other in others:
            total = total + jnp.exp(other - top)
        share = part / total
        high = share.astype(BF16).astype(F32)
        both = jnp.concatenate([high, share - high], axis=0).T.astype(BF16)
        wide = jnp.dot(both, expand, preferred_element_type=F32)
        scaled = (ctx[b].astype(F32) * wide).astype(BF16)

        def columns(k):
            total = None
            for g in range(4):
                block = w[g, 3, k // 2, pl.ds(2 * (k % 2), 2)].reshape(GROUP, GROUP)
                part = jnp.dot(
                    scaled[:, g * GROUP : (g + 1) * GROUP], block, preferred_element_type=F32
                )
                total = part if total is None else total + part
            return total

        away = columns(peers[2]).astype(BF16)
        for way in range(2):
            opp[way, b] = away[way * (BLK // 2) : (way + 1) * (BLK // 2)]
        side[0, b] = columns(peers[1])
        for way in range(2):
            opp_copy(way, b).start()
        side[1, b] = columns(peers[3])
        own[b] = columns(h)

    def attend(b):
        attention_block(b, place, q, kv, ctx, lse_own)
        for d in range(1, 4):
            lse_copy(d, b).start()

    stages = ((finish, 6), (forward, 4), (project, 2), (attend, 0))

    def step(i, state):
        for work, lag in stages:
            b = i - lag

            @pl.when(jnp.logical_and(b >= 0, b < NB))
            def _():
                work(b)

        return state

    lax.fori_loop(0, NB + 6, step, 0)

    def drain(ref, sem):
        pltpu.make_async_copy(ref, ref, sem).wait()

    drain(want.at[pl.ds(0, SHARDS - 1)], req_send)
    drain(stage.at[pl.ds(0, SHARDS - 1)], arr_send)
    for copy in weight_copies:
        copy.wait_send()
    for d in range(3):
        drain(lse_own, lse_send.at[d])
    for way in range(2):
        drain(opp.at[way], opp_send.at[way])
        drain(sendb.at[way], sum_send.at[way])


def whole(place, req, encodings, decoder_states, wq, wk, wv, wo):
    vmem = pl.BlockSpec(memory_space=pltpu.VMEM)
    hbm = pl.BlockSpec(memory_space=pl.ANY)
    dma = pltpu.SemaphoreType.DMA
    return pl.pallas_call(
        kernel,
        out_shape=jax.ShapeDtypeStruct((SEQ_LEN, 256), BF16),
        in_specs=[pl.BlockSpec(memory_space=pltpu.SMEM), vmem] + [hbm] * 6,
        out_specs=vmem,
        scratch_shapes=[
            pltpu.VMEM((SHARDS, NTOK_PART, D), BF16),
            pltpu.VMEM((SEQ_LEN + SPAN_LEN, D), BF16),
            pltpu.VMEM((SHARDS, 1, 128), jnp.int32),
            pltpu.SMEM((SHARDS, 1, 128), jnp.int32),
            pltpu.VMEM((SHARDS, NTOK_PART, D), BF16),
            pltpu.VMEM((SHARDS, NTOK_PART, D), BF16),
            pltpu.VMEM((4, 4, 2, 4, 4, 32, 256), BF16),
            pltpu.VMEM((SEQ_LEN, D), BF16),
            pltpu.VMEM((8, D), F32),
            pltpu.VMEM((8, SHARDS, NTOK_PART, GROUP), BF16),
            pltpu.VMEM((NB, BLK, D), BF16),
            pltpu.VMEM((NB, HEADS, BLK), F32),
            pltpu.VMEM((3, NB, HEADS, BLK), F32),
            pltpu.VMEM((2, NB, BLK // 2, 256), BF16),
            pltpu.VMEM((2, NB, BLK // 2, 256), BF16),
            pltpu.VMEM((2, NB, BLK, 256), F32),
            pltpu.VMEM((NB, BLK, 256), F32),
            pltpu.VMEM((2, NB, BLK, 256), BF16),
            pltpu.VMEM((2, NB, BLK, 256), BF16),
            dma((10,)), dma, dma, dma, dma((SHARDS,)),
            dma((3,)), dma((3,)), dma((3,)), dma((3,)),
            dma((18,)), dma((18,)), dma((18,)), dma((18,)), dma((3,)), dma((3,)),
            dma((3,)), dma((3, NB)), dma((2,)), dma((2, NB)), dma((2,)), dma((2, NB)),
        ],
        compiler_params=pltpu.CompilerParams(
            collective_id=1, has_side_effects=True, vmem_limit_bytes=63 << 20
        ),
        cost_estimate=pl.CostEstimate(
            flops=90_000_000_000, bytes_accessed=16 << 20, transcendentals=1 << 21
        ),
        name="whole",
    )(place, req, encodings, decoder_states, wq, wk, wv, wo)


def body(
    decoder_states, encodings, neighbor_table, query_weight, key_weight, value_weight, out_weight
):
    s = lax.axis_index("span")
    shard_ids = neighbor_table[:, :, 0].reshape(-1)
    slot_ids = neighbor_table[:, :, 1].reshape(-1)
    numbering = jnp.arange(SHARDS, dtype=jnp.int32)
    placed = shard_ids[None, :] == numbering[:, None]
    request = jnp.sum(jnp.where(placed, slot_ids[None, :], 0), axis=1)
    req = jnp.broadcast_to(request[:, None, None], (SHARDS, 1, 128))

    def digits(v):
        return v // 16, (v // 4) % 4, (v // 2) % 2, v % 2

    mine, theirs = digits(s), digits(shard_ids)
    oy, ox, oz, oc = ((a - b + m) % m for a, b, m in zip(mine, theirs, (4, 4, 2, 2)))
    code = ((oy * 4 + ox) * 2 + oz) * 2 + oc
    codes = jnp.array([((o[0] * 4 + o[1]) * 2 + o[2]) * 2 + o[3] for o in OFFSETS], jnp.int32)
    place = jnp.sum(jnp.where(code[:, None] == codes[None, :], numbering[None, :], 0), axis=1)

    sliced = (2, 4, 4, 32, 256)
    summed = whole(
        place, req, encodings, decoder_states,
        query_weight.reshape(sliced), key_weight.reshape(sliced), value_weight.reshape(sliced),
        out_weight.reshape(2, 4, 32, D),
    )
    return jnp.concatenate([jnp.zeros((OFFSET, 256), BF16), summed[: SEQ_LEN - OFFSET]], axis=0)


def solution(mesh):
    return jax.shard_map(
        body,
        mesh=mesh,
        in_specs=(
            P("span", None),
            P("span", "head", None),
            P("span", None, None),
            P(None, "head"),
            P(None, "head"),
            P(None, "head"),
            P("head", None),
        ),
        out_specs=P("span", "head"),
        check_vma=False,
    )
```

time: 344 us -> 218 us (0.63)
  waiting for transfers between devices: 117 us -> 0 us
  Pallas kernels: 101 us -> 208 us
  blocking collectives: 43.7 us -> 0 us
  local copies, waits for them, and re-layouts: 30.7 us -> 4.39 us
  matrix products: 21 us -> 0 us
  between operations: 13.5 us -> 0.03 us
  starting transfers between devices: 9.21 us -> 0 us
    all_gather x1 -> x0, waiting for transfers between devices: 117 us -> none  [body(): whole = lax.all_gather(pieces, 'span', axis=0)]
    pallas_call x1, Pallas kernels: 101 us -> 208 us  [whole(): pl.pallas_call(kernel, out_shape=jax.ShapeDtypeStruct((SEQ_LEN, 256), BF1...]
    all_gather x2 -> x0, blocking collectives: 31 us -> none  [the longest x1 17.3 us: body(): lax.all_gather(jnp.concatenate(column_pieces, axis=0), 'head', axis=1, ti...]
    dot_general x2 -> x0, matrix products: 21 us -> none  [the longest x1 13.2 us: body(): jnp.dot(arrived.reshape(-1, D), both, preferred_element_type=F32)]
    all_to_all x1 -> x0, blocking collectives: 12.6 us -> none  [body(): lax.all_to_all(request, 'span', split_axis=0, concat_axis=0, tiled=True)]
    slice x3 -> x0, local copies, waits for them, and re-layouts: 12.2 us -> none  [the longest x2 6.95 us: body(): whole[:, 48:64].reshape(64, 4, 4, D).transpose(1, 0, 2, 3).reshape(D, D)]
    all_to_all x1 -> x0, starting transfers between devices: 9.21 us -> none  [body(): lax.all_to_all(selected, 'span', split_axis=0, concat_axis=0, tiled=True)]
    another operation x2 -> x0, local copies, waits for them, and re-layouts: 5.6 us -> none  [body(): columns = whole_o.reshape(D, 4, 256).transpose(1, 0, 2)]
  transfers between devices with their start and end apart: 2 -> 0, of which waited for: 1 -> 0; matrix products, arithmetic and copies ran while one was open for 10% -> 0% of each run, Pallas kernels for 0% -> 0%
where the time goes in v3:
time: 218 us; the launch traced here: 214 us
  Pallas kernels  208 us (95%)
  local copies, waits for them, and re-layouts  4.39 us (2%)
    pallas_call x1, Pallas kernels, whole(): pl.pallas_call(kernel, out_shape=jax.ShapeDtypeStruct((SEQ_LEN, 256), BF1...  208 us

profile of v3, /device:TPU:20, one launch (start us, length us, event | category | flops | bytes accessed | tf_op | source)
XLA Modules:
  0.0 214.1 jit_solution(2667163581729244607)
XLA Ops:
  0.0 0.8 fusion.16
  0.8 0.1 copy.14
  0.9 0.1 broadcast_in_dim.33
  1.0 0.1 copy.13
  1.0 0.1 reshape_squeeze.3
  1.2 0.1 select_reduce_fusion
  1.3 1.4 select_reduce_fusion.1.place
  2.7 0.7 broadcast_in_dim.35.req
  3.5 208.1 %whole.1 = bf16[2048,256]{1,0:T(8,128)(2,1)} custom-call(s32[64]{0:T(128)} %select_reduce_fusion.1.place, s32[64,1,128]{2,1,0:T(1,128)} %broadcast_in_dim.35.req, bf16[64,32,1024]{2,1,0:T(8,128)(2,1)} %enc_hbm.1, bf16[2048,1024]{1,0:T(8,128)(2,1)} %dec_hbm.1, bf16[2,4,4,32,256]{4,3,2,1,0:T(8,128)(2,1)} %bitcast.8, bf16[2,4,4,32,256]{4,3,2,1,0:T(8,128)(2,1)} %bitcast.9, ...), custom_call_target="tpu_custom_call" | custom-call | flops 89999998976 | bytes 16777216 | tf_op jit(solution)/shard_map/whole/pallas_call | solution.py:388
  211.6 1.3 slice.11
  212.9 1.2 concatenate.3
  (1 shorter events, 0.0 us)

commit v4 on v3

--- a/solution.py
+++ b/solution.py
@@ -15,7 +15,6 @@
 SPANS = 32
 SHARDS = 64
 NTOK_PART = 32
-OFFSET = SPAN_LEN - 1
 GROUP = 256
 BLK = 128
 NB = SEQ_LEN // BLK
@@ -25,21 +24,29 @@
 MESH = pl.DeviceIdType.MESH
 
 
-def far(o):
-    return min(o[0], 4 - o[0]) + min(o[1], 4 - o[1]) + o[2]
-
-
-OFFSETS = [(0, 0, 0, 0)] + sorted(
-    [
-        (oy, ox, oz, oc)
-        for oy in range(4)
-        for ox in range(4)
-        for oz in range(2)
-        for oc in range(2)
-        if (oy, ox, oz, oc) != (0, 0, 0, 0)
-    ],
-    key=lambda o: -far(o),
-)
+def links(o):
+    ways = ((0, 0), (1, 0), (1, 1), (0, 1))
+    return [*ways[o[1]], *ways[o[0]], o[2]]
+
+
+def balanced(offsets):
+    left, done, order = list(offsets), [0] * 5, []
+    while left:
+
+        def cost(o):
+            after = [a + b for a, b in zip(done, links(o))]
+            mean = sum(after) / 5
+            return sum((v - mean) ** 2 for v in after) - sum(links(o))
+
+        best = min(left, key=cost)
+        left.remove(best)
+        order.append(best)
+        done = [a + b for a, b in zip(done, links(best))]
+    return order
+
+
+ALL = [(oy, ox, oz, oc) for oy in range(4) for ox in range(4) for oz in range(2) for oc in range(2)]
+OFFSETS = ALL[:1] + balanced(ALL[1:])
 
 
 def head_mask(rows, cols):
@@ -57,8 +64,8 @@
     stats = []
     for sp in range(BLK // SPAN_LEN):
         j = b * (BLK // SPAN_LEN) + sp
-        first = place[2 * j]
-        second = place[2 * j + 1]
+        first = place(2 * j)
+        second = place(2 * j + 1)
         rows = pl.ds(pl.multiple_of(j * SPAN_LEN, SPAN_LEN), SPAN_LEN)
         lses = jnp.zeros((SPAN_LEN, 128), F32)
         for g in range(D // GROUP):
@@ -89,8 +96,8 @@
 
 
 def kernel(
-    place, req, enc_hbm, dec_hbm, wq, wk, wv, wo, out,
-    enc, dec, want, want_s, stage, arr, w, q, carry, kv,
+    table, position, enc_hbm, dec_hbm, wq, wk, wv, wo, out,
+    enc, dec, req, want, want_s, stage, arr, w, q, carry, kv,
     ctx, lse_own, lse_in, opp, opp_in, side, own, sendb, sum_in,
     load_sem, req_send, req_recv, arr_send, arr_recv,
     z_send, z_recv, a_send, a_recv, one_send, one_recv, two_send, two_recv, c_send, c_recv,
@@ -119,7 +126,7 @@
 
     loads = [
         pltpu.make_async_copy(src, w.at[h, i], load_sem.at[i])
-        for i, src in enumerate((wq, wk, wv))
+        for i, src in ((0, wk), (1, wq), (2, wv))
     ] + [
         pltpu.make_async_copy(
             wo.at[:, :, :, k * 256 : (k + 1) * 256],
@@ -140,6 +147,11 @@
         pl.semaphore_signal(barrier, inc=1, device_id={"span": target(o)}, device_id_type=MESH)
     for d in range(1, 4):
         pl.semaphore_signal(barrier, inc=1, device_id={"head": peers[d]}, device_id_type=MESH)
+    shard_row = lax.broadcasted_iota(jnp.int32, (SHARDS, 128), 0)
+    slots = jnp.zeros((SHARDS, 128), jnp.int32)
+    for e in range(SHARDS):
+        slots = jnp.where(shard_row == table[2 * e], table[2 * e + 1], slots)
+    req[...] = slots.reshape(SHARDS, 1, 128)
     want[s] = req[s]
     dec[SEQ_LEN:] = jnp.zeros((SPAN_LEN, D), BF16)
     pl.semaphore_wait(barrier, SHARDS - 1 + 3)
@@ -150,38 +162,37 @@
 
     def z_copy(d):
         piece = w.at[h, :, core, y, x, pl.ds(pl.multiple_of(zl * 16, 16), 16), :]
-        return send(piece, piece, z_send.at[d - 1], z_recv.at[d - 1], {"head": peers[d]})
+        return send(piece, piece, z_send, z_recv.at[d - 1], {"head": peers[d]})
 
     def a_copy(d):
         piece = w.at[peers[d], :, core, y, x, pl.ds(pl.multiple_of(zl * 16, 16), 16), :]
         to = {"span": index(y, x, 1 - zl, core)}
-        return send(piece, piece, a_send.at[d - 1], a_recv.at[d - 1], to)
+        return send(piece, piece, a_send, a_recv.at[d - 1], to)
 
     def one_copy(half, e, d):
         piece = w.at[peers[d], 2 * half : 2 * half + 2, core, y, x]
         to = index(y, (x + e) % 4, zl, core) if half == 0 else index((y + e) % 4, x, zl, core)
         n = (half * 3 + e - 1) * 3 + d - 1
-        return send(piece, piece, one_send.at[n], one_recv.at[n], {"span": to})
-
-    def two_copy(half, e, d):
+        return send(piece, piece, one_send, one_recv.at[n], {"span": to})
+
+    def two_copy(group, half, e, d):
         if half == 0:
-            piece = w.at[peers[d], 0:2, core, y]
+            piece = w.at[peers[d], group, core, y]
             to = index((y + e) % 4, x, zl, core)
         else:
-            piece = w.at[peers[d], 2:4, core, :, x]
+            piece = w.at[peers[d], 2 + group, core, :, x]
             to = index(y, (x + e) % 4, zl, core)
-        n = (half * 3 + e - 1) * 3 + d - 1
-        return send(piece, piece, two_send.at[n], two_recv.at[n], {"span": to})
-
-    def c_copy(d):
-        piece = w.at[peers[d], :, core]
-        return send(piece, piece, c_send.at[d - 1], c_recv.at[d - 1], {"span": index(y, x, zl, 1 - core)})
+        n = ((group * 2 + half) * 3 + e - 1) * 3 + d - 1
+        return send(piece, piece, two_send.at[group], two_recv.at[n], {"span": to})
+
+    def c_copy(group, half, d):
+        piece = w.at[peers[d], 2 * half + group, core]
+        n = (group * 2 + half) * 3 + d - 1
+        to = {"span": index(y, x, zl, 1 - core)}
+        return send(piece, piece, c_send.at[group], c_recv.at[n], to)
 
     ring = [(half, e, d) for e in (1, 2, 3) for d in (1, 2, 3) for half in (0, 1)]
-    weight_copies = [z_copy(d) for d in (1, 2, 3)] + [a_copy(d) for d in (1, 2, 3)]
-    weight_copies += [one_copy(*r) for r in ring] + [two_copy(*r) for r in ring]
-    weight_copies += [c_copy(d) for d in (1, 2, 3)]
-
+    swap = [(half, d) for d in (1, 2, 3) for half in (0, 1)]
     def arr_copy(i):
         to = {"span": target(OFFSETS[i])}
         return send(stage.at[i], arr.at[i], arr_send, arr_recv.at[i], to)
@@ -214,27 +225,57 @@
         a_copy(d).wait_recv()
     for r in ring:
         one_copy(*r).start()
-    issue(9, 17)
+    issue(9, 13)
     for r in ring:
         one_copy(*r).wait_recv()
     for r in ring:
-        two_copy(*r).start()
-    issue(17, SHARDS)
+        two_copy(0, *r).start()
+    issue(13, 21)
+    for r in ring:
+        two_copy(0, *r).wait_recv()
+    for r in swap:
+        c_copy(0, *r).start()
+    issue(21, 37)
+    for r in ring:
+        two_copy(1, *r).start()
+    issue(37, SHARDS)
     arr[0] = enc[want_s[s, 0, 0]]
     arr_copy(SHARDS - 1).start()
-    for r in ring:
-        two_copy(*r).wait_recv()
-    for d in (1, 2, 3):
-        c_copy(d).start()
-    dec_load.wait()
-    for d in (1, 2, 3):
-        c_copy(d).wait_recv()
+    for r in swap:
+        c_copy(0, *r).wait_recv()
 
     def weight(group, i):
         return w[group, i].reshape(D, GROUP)
 
+    def project_chunk(k, state):
+        for i in range(8):
+            n = 8 * k + i
+
+            @pl.when(n > 0)
+            def _():
+                send(stage.at[n], arr.at[n], arr_send, arr_recv.at[n], {"span": s}).wait_recv()
+
+        tokens = arr[pl.ds(8 * k, 8)].reshape(8 * NTOK_PART, D)
+
+        def columns(n, inner):
+            part = jnp.dot(tokens, weight(n % 4, 2 * (n // 4)), preferred_element_type=F32)
+            kv[n, pl.ds(8 * k, 8)] = part.astype(BF16).reshape(8, NTOK_PART, GROUP)
+            return inner
+
+        return lax.fori_loop(0, 8, columns, state)
+
+    lax.fori_loop(0, 4, project_chunk, 0)
+    for r in ring:
+        two_copy(1, *r).wait_recv()
+    for r in swap:
+        c_copy(1, *r).start()
+    lax.fori_loop(4, 6, project_chunk, 0)
+    dec_load.wait()
+    for r in swap:
+        c_copy(1, *r).wait_recv()
+
     for g in range(4):
-        head_rows = jnp.dot(dec[48:64], weight(g, 0), preferred_element_type=F32)
+        head_rows = jnp.dot(dec[48:64], weight(g, 1), preferred_element_type=F32)
         carry[:, g * GROUP : (g + 1) * GROUP] = head_rows[8:16]
 
     first_row = lax.broadcasted_iota(jnp.int32, (QT, GROUP), 0) == 0
@@ -243,7 +284,7 @@
         source = dec[pl.ds(pl.multiple_of(t * QT + 64, 64), QT)]
         for g in range(4):
             cols = slice(g * GROUP, (g + 1) * GROUP)
-            tile = jnp.dot(source, weight(g, 0), preferred_element_type=F32)
+            tile = jnp.dot(source, weight(g, 1), preferred_element_type=F32)
             before = carry[7:8, cols]
             moved = jnp.where(first_row, before, pltpu.roll(tile, 1, 0))
             q[pl.ds(pl.multiple_of(t * QT, QT), QT), cols] = moved.astype(BF16)
@@ -252,24 +293,7 @@
 
     lax.fori_loop(0, SEQ_LEN // QT, query_tile, 0)
 
-    def project_chunk(k, state):
-        for i in range(8):
-            n = 8 * k + i
-
-            @pl.when(n > 0)
-            def _():
-                send(stage.at[n], arr.at[n], arr_send, arr_recv.at[n], {"span": s}).wait_recv()
-
-        tokens = arr[pl.ds(8 * k, 8)].reshape(8 * NTOK_PART, D)
-
-        def columns(n, inner):
-            part = jnp.dot(tokens, weight(n % 4, 1 + n // 4), preferred_element_type=F32)
-            kv[n, pl.ds(8 * k, 8)] = part.astype(BF16).reshape(8, NTOK_PART, GROUP)
-            return inner
-
-        return lax.fori_loop(0, 8, columns, state)
-
-    lax.fori_loop(0, SHARDS // 8, project_chunk, 0)
+    lax.fori_loop(6, SHARDS // 8, project_chunk, 0)
 
     def lse_copy(d, b):
         return send(
@@ -296,9 +320,23 @@
     def finish(b):
         for way in range(2):
             sum_copy(way, b).wait_recv()
-        rows = pl.ds(pl.multiple_of(b * BLK, BLK), BLK)
         total = own[b] + (sum_in[0, b].astype(F32) + sum_in[1, b].astype(F32))
-        out[rows, :] = total.astype(BF16)
+        own[b] = total
+
+        @pl.when(b == 0)
+        def _():
+            last = lax.broadcasted_iota(jnp.int32, (SPAN_LEN, 256), 0) == SPAN_LEN - 1
+            out[:SPAN_LEN] = jnp.where(last, total[0:1], 0.0).astype(BF16)
+
+        @pl.when(b > 0)
+        def _():
+            last = lax.broadcasted_iota(jnp.int32, (BLK, 256), 0) == BLK - 1
+            moved = jnp.where(last, total[0:1], pltpu.roll(own[b - 1], BLK - 1, 0))
+            out[pl.ds(pl.multiple_of((b - 1) * BLK + SPAN_LEN, SPAN_LEN), BLK)] = moved.astype(BF16)
+
+        @pl.when(b == NB - 1)
+        def _():
+            out[SEQ_LEN - SPAN_LEN :] = pltpu.roll(total, BLK - 1, 0)[:SPAN_LEN].astype(BF16)
 
     def forward(b):
         half = BLK // 2
@@ -348,6 +386,12 @@
         side[1, b] = columns(peers[3])
         own[b] = columns(h)
 
+    def place(e):
+        shard = table[2 * e]
+        oy, ox = (y + 4 - shard // 16) % 4, (x + 4 - (shard // 4) % 4) % 4
+        oz, oc = (zl + 2 - (shard // 2) % 2) % 2, (core + 2 - shard % 2) % 2
+        return position[index(oy, ox, oz, oc)]
+
     def attend(b):
         attention_block(b, place, q, kv, ctx, lse_own)
         for d in range(1, 4):
@@ -372,8 +416,12 @@
 
     drain(want.at[pl.ds(0, SHARDS - 1)], req_send)
     drain(stage.at[pl.ds(0, SHARDS - 1)], arr_send)
-    for copy in weight_copies:
-        copy.wait_send()
+    drain(kv.at[0, 0:6], z_send)
+    drain(kv.at[0, 0:6], a_send)
+    drain(kv.at[0, 0:36], one_send)
+    for group in (0, 1):
+        drain(kv.at[0:2, 0:36], two_send.at[group])
+        drain(kv.at[0:2, 0:48], c_send.at[group])
     for d in range(3):
         drain(lse_own, lse_send.at[d])
     for way in range(2):
@@ -381,18 +429,19 @@
         drain(sendb.at[way], sum_send.at[way])
 
 
-def whole(place, req, encodings, decoder_states, wq, wk, wv, wo):
+def whole(table, position, encodings, decoder_states, wq, wk, wv, wo):
     vmem = pl.BlockSpec(memory_space=pltpu.VMEM)
     hbm = pl.BlockSpec(memory_space=pl.ANY)
     dma = pltpu.SemaphoreType.DMA
     return pl.pallas_call(
         kernel,
         out_shape=jax.ShapeDtypeStruct((SEQ_LEN, 256), BF16),
-        in_specs=[pl.BlockSpec(memory_space=pltpu.SMEM), vmem] + [hbm] * 6,
+        in_specs=[pl.BlockSpec(memory_space=pltpu.SMEM)] * 2 + [hbm] * 6,
         out_specs=vmem,
         scratch_shapes=[
             pltpu.VMEM((SHARDS, NTOK_PART, D), BF16),
             pltpu.VMEM((SEQ_LEN + SPAN_LEN, D), BF16),
+            pltpu.VMEM((SHARDS, 1, 128), jnp.int32),
             pltpu.VMEM((SHARDS, 1, 128), jnp.int32),
             pltpu.SMEM((SHARDS, 1, 128), jnp.int32),
             pltpu.VMEM((SHARDS, NTOK_PART, D), BF16),
@@ -411,8 +460,7 @@
             pltpu.VMEM((2, NB, BLK, 256), BF16),
             pltpu.VMEM((2, NB, BLK, 256), BF16),
             dma((10,)), dma, dma, dma, dma((SHARDS,)),
-            dma((3,)), dma((3,)), dma((3,)), dma((3,)),
-            dma((18,)), dma((18,)), dma((18,)), dma((18,)), dma((3,)), dma((3,)),
+            dma, dma((3,)), dma, dma((3,)), dma, dma((18,)), dma((2,)), dma((36,)), dma((2,)), dma((12,)),
             dma((3,)), dma((3, NB)), dma((2,)), dma((2, NB)), dma((2,)), dma((2, NB)),
         ],
         compiler_params=pltpu.CompilerParams(
@@ -422,36 +470,21 @@
             flops=90_000_000_000, bytes_accessed=16 << 20, transcendentals=1 << 21
         ),
         name="whole",
-    )(place, req, encodings, decoder_states, wq, wk, wv, wo)
+    )(table, position, encodings, decoder_states, wq, wk, wv, wo)
 
 
 def body(
     decoder_states, encodings, neighbor_table, query_weight, key_weight, value_weight, out_weight
 ):
-    s = lax.axis_index("span")
-    shard_ids = neighbor_table[:, :, 0].reshape(-1)
-    slot_ids = neighbor_table[:, :, 1].reshape(-1)
-    numbering = jnp.arange(SHARDS, dtype=jnp.int32)
-    placed = shard_ids[None, :] == numbering[:, None]
-    request = jnp.sum(jnp.where(placed, slot_ids[None, :], 0), axis=1)
-    req = jnp.broadcast_to(request[:, None, None], (SHARDS, 1, 128))
-
-    def digits(v):
-        return v // 16, (v // 4) % 4, (v // 2) % 2, v % 2
-
-    mine, theirs = digits(s), digits(shard_ids)
-    oy, ox, oz, oc = ((a - b + m) % m for a, b, m in zip(mine, theirs, (4, 4, 2, 2)))
-    code = ((oy * 4 + ox) * 2 + oz) * 2 + oc
-    codes = jnp.array([((o[0] * 4 + o[1]) * 2 + o[2]) * 2 + o[3] for o in OFFSETS], jnp.int32)
-    place = jnp.sum(jnp.where(code[:, None] == codes[None, :], numbering[None, :], 0), axis=1)
+    codes = [((o[0] * 4 + o[1]) * 2 + o[2]) * 2 + o[3] for o in OFFSETS]
+    position = jnp.array([codes.index(code) for code in range(SHARDS)], jnp.int32)
 
     sliced = (2, 4, 4, 32, 256)
-    summed = whole(
-        place, req, encodings, decoder_states,
+    return whole(
+        neighbor_table.reshape(-1), position, encodings, decoder_states,
         query_weight.reshape(sliced), key_weight.reshape(sliced), value_weight.reshape(sliced),
         out_weight.reshape(2, 4, 32, D),
     )
-    return jnp.concatenate([jnp.zeros((OFFSET, 256), BF16), summed[: SEQ_LEN - OFFSET]], axis=0)
 
 
 def solution(mesh):

time: 218 us -> 200 us (0.917); the launches traced: 214 us -> 200 us
  Pallas kernels: 208 us -> 196 us
    pallas_call x1, Pallas kernels: 208 us -> 196 us  [whole(): pl.pallas_call(kernel, out_shape=jax.ShapeDtypeStruct((SEQ_LEN, 256), BF1...]
    unnamed x0 -> x2, local copies, waits for them, and re-layouts: none -> 3.04 us
    slice x4 -> x0, local copies, waits for them, and re-layouts: 2.22 us -> none  [the longest x1 1.28 us: body(): summed[:SEQ_LEN - OFFSET]]
where the time goes in v4:
time: 200 us
  Pallas kernels  196 us (98%)
  local copies, waits for them, and re-layouts  3.7 us (2%)
    pallas_call x1, Pallas kernels, whole(): pl.pallas_call(kernel, out_shape=jax.ShapeDtypeStruct((SEQ_LEN, 256), BF1...  196 us

profile of v4, /device:TPU:20, one launch (start us, length us, event | category | flops | bytes accessed | tf_op | source)
XLA Modules:
  0.0 199.9 jit_solution(6746504619566908446)
XLA Ops:
  0.0 0.8 copy.10
  0.8 0.7 reshape.15.table
  1.4 196.2 %whole.1 = bf16[2048,256]{1,0:T(8,128)(2,1)} custom-call(s32[128]{0:T(128)} %reshape.15.table, s32[64]{0:T(128)} %constant.2.clone.position, bf16[64,32,1024]{2,1,0:T(8,128)(2,1)} %enc_hbm.1, bf16[2048,1024]{1,0:T(8,128)(2,1)} %dec_hbm.1, bf16[2,4,4,32,256]{4,3,2,1,0:T(8,128)(2,1)} %bitcast.4, bf16[2,4,4,32,256]{4,3,2,1,0:T(8,128)(2,1)} %bitcast.5, ...), custom_call_target="tpu_custom_call" | custom-call | flops 89999998976 | bytes 16777216 | tf_op jit(solution)/shard_map/whole/pallas_call | solution.py:436
  197.7 2.3 %copy.12 = bf16[2048,256]{1,0:T(8,128)(2,1)} copy(bf16[2048,256]{1,0:T(8,128)(2,1)} %whole.1) | data formatting | bytes 2097152

commit v5 on v4

--- a/solution.py
+++ b/solution.py
@@ -397,7 +397,7 @@
         for d in range(1, 4):
             lse_copy(d, b).start()
 
-    stages = ((finish, 6), (forward, 4), (project, 2), (attend, 0))
+    stages = ((finish, 8), (forward, 5), (project, 2), (attend, 0))
 
     def step(i, state):
         for work, lag in stages:
@@ -409,7 +409,7 @@
 
         return state
 
-    lax.fori_loop(0, NB + 6, step, 0)
+    lax.fori_loop(0, NB + 8, step, 0)
 
     def drain(ref, sem):
         pltpu.make_async_copy(ref, ref, sem).wait()

time: 200 us -> 202 us (1.010)
  no operation moved by 1% of the time
where the time goes in v5:
time: 202 us
  Pallas kernels  198 us (98%)
  local copies, waits for them, and re-layouts  3.7 us (2%)
    pallas_call x1, Pallas kernels, whole(): pl.pallas_call(kernel, out_shape=jax.ShapeDtypeStruct((SEQ_LEN, 256), BF1...  198 us

profile of v5, /device:TPU:20, one launch (start us, length us, event | category | flops | bytes accessed | tf_op | source)
XLA Modules:
  0.0 201.8 jit_solution(13079041487347613847)
XLA Ops:
  0.0 0.8 copy.10
  0.8 0.7 reshape.15.table
  1.4 198.1 %whole.1 = bf16[2048,256]{1,0:T(8,128)(2,1)} custom-call(s32[128]{0:T(128)} %reshape.15.table, s32[64]{0:T(128)} %constant.2.clone.position, bf16[64,32,1024]{2,1,0:T(8,128)(2,1)} %enc_hbm.1, bf16[2048,1024]{1,0:T(8,128)(2,1)} %dec_hbm.1, bf16[2,4,4,32,256]{4,3,2,1,0:T(8,128)(2,1)} %bitcast.4, bf16[2,4,4,32,256]{4,3,2,1,0:T(8,128)(2,1)} %bitcast.5, ...), custom_call_target="tpu_custom_call" | custom-call | flops 89999998976 | bytes 16777216 | tf_op jit(solution)/shard_map/whole/pallas_call | solution.py:436
  199.6 2.3 %copy.12 = bf16[2048,256]{1,0:T(8,128)(2,1)} copy(bf16[2048,256]{1,0:T(8,128)(2,1)} %whole.1) | data formatting | bytes 2097152
